TPU v7x, 128 devices: a whole 4x4x4 slice. The times are simulated.
128 devices in a mesh: grid: 16 (over y, z_lo, core), dom: 8 (over x, z_hi).
Axes of the slice: x: 4, y: 4, z: 4 (z_hi: 2, z_lo: 2; z = z_hi * 2 + z_lo), core: 2. Of those that a mesh axis runs over, the one named last changes fastest.
Arguments:
- values: float32 [16, 32, 4, 4, 8, 8, 128], P('grid', 'dom'), may hold values from -2 to 2
- levels: int32 [16, 6], P('grid'), may hold values from 0 to 7, as said below
- coefficients: int32 [16], P('grid'), may hold values from -3 to 3, as said below
Outputs:
- combined: float32 [16, 32, 4, 4, 8, 8, 128], P('grid', 'dom')
Inputs may be any that keep to these rules, and one draw needn't show every extreme that they name: levels[g, k] is grid g's level along dimension k + 1. With L_k the base-two logarithm of that dimension's extent (32, 4, 4, 8, 8, 128), each entry lies between L_k - 2 and L_k, and the shortfalls L_k - levels[g, k] of one grid add up to 2 at most. `coefficients`: every coefficient is nonzero.
All inputs are finite; a program needn't handle non-finite values.
Results may differ from a plain program's by a relative error of at most 0.0003.
Values sent between devices are 32-bit elements; how exact they have to be, the bound alone decides.
No kernel may reach another device: no remote copies, remote signals or barrier semaphores. Data moves between devices by JAX's collectives and lax.ppermute only.
A program may use at most 64 MiB of HBM per device.

v0:
```python
import jax
import jax.numpy as jnp
import numpy as np
from jax import lax
from jax.experimental import pallas as pl
from jax.experimental.pallas import tpu as pltpu
from jax.sharding import PartitionSpec as P


TOPS = (5, 2, 2, 3, 3, 7)


def coarse_position(numerator, level_now):
    while numerator > 0 and numerator % 2 == 0:
        numerator = numerator // 2
        level_now = level_now - 1
    if numerator == 0:
        return 0
    return (1 << (level_now - 1)) + (numerator - 1) // 2


def parent_positions(position):
    level_now = position.bit_length()
    span_size = 1 << (level_now - 1)
    offset = position - span_size
    return [
        coarse_position(offset % span_size, level_now - 1),
        coarse_position((offset + 1) % span_size, level_now - 1),
    ]


def interp_tables(top):
    points = 1 << top
    result = []
    for short in range(3):
        matrix = np.eye(points)
        for position in range(points >> short, points):
            first, second = parent_positions(position)
            matrix[position] = 0.5 * (matrix[first] + matrix[second])
        result.append(matrix)
    return np.stack(result)


def two_sources(tables):
    sources = np.zeros((2, *tables.shape[:2]), dtype=np.int32)
    weights = np.zeros((2, *tables.shape[:2]), dtype=np.float32)
    for short in range(tables.shape[0]):
        for row in range(tables.shape[1]):
            found = np.nonzero(tables[short, row])[0]
            for i in range(2):
                at = found[min(i, len(found) - 1)]
                sources[i, short, row] = at
                weights[i, short, row] = tables[short, row, at] if i < len(found) else 0.0
    return sources, weights


def by_shortfall(table, short):
    sublane = lax.broadcasted_iota(jnp.int32, (8, 128), 0)
    kind = np.asarray(table).dtype.type
    result = jnp.full((8, 128), kind(0))
    for row in range(8):
        per = [kind(table[i, row]) for i in range(3)]
        here = jnp.where(short == 0, per[0], jnp.where(short == 1, per[1], per[2]))
        result = jnp.where(sublane == row, here, result)
    return result


def lead_interp(values, top, short):
    result = list(values)
    points = 1 << top
    for missing in (2, 1):
        for position in range(points >> missing, points >> (missing - 1)):
            first, second = parent_positions(position)
            if first == second:
                mean = result[first]
            else:
                mean = 0.5 * (result[first] + result[second])
            result[position] = jnp.where(short >= missing, mean, result[position])
    return result


def interp_kernel(levels, coefs, x, pf, *rest):
    keep, send = rest[-2:]
    core = lax.rem(lax.axis_index("grid"), 2)
    weight = coefs[0].astype(jnp.float32)
    short = [TOPS[k] - levels[0, k] for k in range(6)]
    matrix = pf[short[5]]
    rows = x[0, 0].reshape(1024, 128)
    high = rows.astype(jnp.bfloat16)
    low = (rows - high.astype(jnp.float32)).astype(jnp.bfloat16)
    along_f = jnp.dot(high, matrix, preferred_element_type=jnp.float32) + jnp.dot(
        low, matrix, preferred_element_type=jnp.float32
    )
    tiles = along_f.reshape(16, 8, 8, 128)
    sources, weights = two_sources(interp_tables(3))
    src1, src2 = (by_shortfall(sources[i], short[4]) for i in range(2))
    wt1, wt2 = (by_shortfall(weights[i], short[4]) * weight for i in range(2))
    done = []
    for bc in range(16):
        along_e = []
        for d in range(8):
            tile = tiles[bc, d]
            along_e.append(
                wt1 * jnp.take_along_axis(tile, src1, axis=0) + wt2 * jnp.take_along_axis(tile, src2, axis=0)
            )
        done.append(lead_interp(along_e, 3, short[3]))
    for d in range(8):
        grid_now = [[done[b * 4 + c][d] for c in range(4)] for b in range(4)]
        grid_now = [lead_interp(line, 2, short[2]) for line in grid_now]
        columns = [lead_interp([grid_now[b][c] for b in range(4)], 2, short[1]) for c in range(4)]
        for b in range(4):
            for half in range(2):
                even, odd = columns[2 * half][b], columns[2 * half + 1][b]
                at = b * 2 + half
                keep[at, 0, d] = jnp.where(core == 0, even, odd)
                send[at, 0, d] = jnp.where(core == 0, odd, even)


def in_vmem(x):
    return pltpu.with_memory_space_constraint(x, pltpu.VMEM)


def in_hbm(x):
    return pltpu.with_memory_space_constraint(x, pltpu.HBM)


def interp_rows(values, levels, coefs, matrices, first, count, after=()):
    smem = pl.BlockSpec(memory_space=pltpu.SMEM)
    half = jax.ShapeDtypeStruct((8, count, 8, 8, 128), jnp.float32)
    out_spec = pl.BlockSpec((8, 1, 8, 8, 128), lambda a: (0, a, 0, 0, 0))
    return pl.pallas_call(
        interp_kernel,
        grid=(count,),
        in_specs=[
            smem,
            smem,
            pl.BlockSpec((1, 1, 4, 4, 8, 8, 128), lambda a: (0, a + first, 0, 0, 0, 0, 0)),
            pl.BlockSpec((3, 128, 128), lambda a: (0, 0, 0)),
            *[pl.BlockSpec(memory_space=pl.ANY) for _ in after],
        ],
        out_specs=[out_spec, out_spec],
        out_shape=[half, half],
        compiler_params=pltpu.CompilerParams(vmem_limit_bytes=16 << 20),
        cost_estimate=pl.CostEstimate(flops=count * 10**8, bytes_accessed=count << 20, transcendentals=0),
    )(in_hbm(levels), coefs, in_hbm(values), in_hbm(matrices), *after)


def combine_kernel(levels, others, own0, own123, got0, got123, next_own, next_got, out):
    short = TOPS[0] - levels[0, 0]
    other_short = TOPS[0] - others[0, 0]
    for at in range(8):
        for d in range(8):
            total = None
            for zero, rest, after, miss in (
                (own0, own123, next_own, short),
                (got0, got123, next_got, other_short),
            ):
                start, end = zero[at, 0, d], after[at, 0, d]
                one, two, three = (rest[at, i, d] for i in range(3))
                two = jnp.where(miss >= 2, 0.5 * (start + end), two)
                one = jnp.where(miss >= 1, 0.5 * (start + two), one)
                three = jnp.where(miss >= 1, 0.5 * (two + end), three)
                part = (start, one, two, three)
                total = part if total is None else tuple(s + t for s, t in zip(total, part))
            for i in range(4):
                out[at, i, d] = total[i]


def combine(levels, others, *pieces):
    smem = pl.BlockSpec(memory_space=pltpu.SMEM)
    vmem = pl.BlockSpec(memory_space=pltpu.VMEM)
    return pl.pallas_call(
        combine_kernel,
        in_specs=[smem, smem, *[vmem] * len(pieces)],
        out_specs=vmem,
        out_shape=pltpu.VMEM((8, 4, 8, 8, 128), jnp.float32),
        compiler_params=pltpu.CompilerParams(vmem_limit_bytes=4 << 20),
        name="combine",
    )(levels, others, *[in_vmem(p) for p in pieces])


def restrict_kernel(levels, *refs):
    pieces, out, scratch, sems = refs[:16], *refs[16:]
    index = lax.axis_index("grid")
    short = [TOPS[k] - levels[0, k] for k in range(6)]
    spacing = jnp.left_shift(jnp.int32(1), short[0])
    sublane = lax.broadcasted_iota(jnp.int32, (8, 128), 0)
    lane = lax.broadcasted_iota(jnp.int32, (8, 128), 1)
    inside = (sublane < jnp.right_shift(8, short[4])) & (lane < jnp.right_shift(128, short[5]))
    tile = jnp.where(inside, 1.0, 0.0)
    by_d = [jnp.where(d < jnp.right_shift(8, short[3]), tile, 0.0) for d in range(8)]
    copies = []
    for row in range(4):
        held_a = jnp.where(lax.rem(jnp.int32(row), spacing) == 0, 1.0, 0.0)
        for slot, piece in enumerate(pieces):
            at = index ^ slot
            b, c = jnp.right_shift(at, 2), at & 3
            held = jnp.where(
                (b < jnp.right_shift(4, short[1])) & (c < jnp.right_shift(4, short[2])), held_a, 0.0
            )
            for d in range(8):
                scratch[row, at, d] = piece[row, d] * (by_d[d] * held)
        copies.append(pltpu.make_async_copy(scratch.at[row], out.at[row], sems.at[row]))
        copies[-1].start()
    for copy in copies:
        copy.wait()


def restrict(levels, pieces):
    out = pl.pallas_call(
        restrict_kernel,
        in_specs=[pl.BlockSpec(memory_space=pltpu.SMEM)] + [pl.BlockSpec(memory_space=pltpu.VMEM)] * 16,
        out_specs=pl.BlockSpec(memory_space=pl.ANY),
        out_shape=jax.ShapeDtypeStruct((4, 16, 8, 8, 128), jnp.float32),
        scratch_shapes=[pltpu.VMEM((4, 16, 8, 8, 128), jnp.float32), pltpu.SemaphoreType.DMA((4,))],
        compiler_params=pltpu.CompilerParams(vmem_limit_bytes=4 << 20),
        name="restrict",
    )(levels, *[in_vmem(p) for p in pieces])
    return out.reshape(1, 4, 4, 4, 8, 8, 128)


def swap(x, bits):
    return lax.ppermute(x, "grid", [(i, i ^ bits) for i in range(16)])


def to_previous(x, bits):
    pairs = [(r * 8 + d, (r ^ bits) * 8 + (d - 1) % 8) for r in range(16) for d in range(8)]
    return lax.ppermute(x, ("grid", "dom"), pairs)


def whole(values, levels, coefficients):
    matrices = jnp.asarray(interp_tables(7).transpose(0, 2, 1), dtype=jnp.bfloat16)
    others = swap(levels, 1)
    keep0, send0 = interp_rows(values, levels, coefficients, matrices, 0, 1)
    next_own = to_previous(keep0, 0)
    next_got = to_previous(send0, 1)
    keep123, send123 = interp_rows(values, levels, coefficients, matrices, 1, 3, (keep0,))
    got0, got123 = swap(send0, 1), swap(send123, 1)
    parts = combine(levels, others, keep0, keep123, got0, got123, next_own, next_got)
    groups = [[h * 2 + core for h in range(8)] for core in range(2)]
    arrived = lax.all_to_all(parts, "grid", split_axis=0, concat_axis=0, axis_index_groups=groups, tiled=True)
    share = arrived.sum(axis=0)
    pieces = {0: share}
    for bits in (4, 12, 2, 6, 14, 8, 10):
        pieces[bits] = swap(share, bits)
    for bits in list(pieces):
        pieces[bits + 1] = swap(pieces[bits], 1)
    return restrict(levels, [pieces[slot] for slot in range(16)])


def solution(mesh):
    in_specs = (P("grid", "dom", None, None, None, None, None), P("grid", None), P("grid"))
    out_specs = P("grid", "dom", None, None, None, None, None)
    return jax.shard_map(whole, mesh=mesh, in_specs=in_specs, out_specs=out_specs, check_vma=False)
```

profile of v0, /device:TPU:1, one launch (start us, length us, event | category | flops | bytes accessed | tf_op | source)
XLA Modules:
  0.0 67.5 jit_solution(8607803676727311984)
XLA Ops:
  0.7 0.0 copy-start
  0.7 1.4 %shard_map.46 = (f32[8,1,8,8,128]{4,3,2,1,0:T(8,128)S(1)}, f32[8,1,8,8,128]{4,3,2,1,0:T(8,128)S(1)}) custom-call(s32[1,6]{1,0:T(1,128)} %levels.7, s32[1]{0:T(128)S(6)} %copy.5.coefs, f32[1,4,4,4,8,8,128]{6,5,4,3,2,1,0:T(8,128)} %x.3, bf16[3,128,128]{2,1,0:T(8,128)(2,1)} %constant.4.clone.pf), custom_call_target="tpu_custom_call" | custom-call | flops 100000000 | bytes 1048576 | tf_op jit(solution)/shard_map/pallas_call | solution.py:131
  2.1 3.0 %shard_map.47 = (f32[8,3,8,8,128]{4,3,2,1,0:T(8,128)S(1)}, f32[8,3,8,8,128]{4,3,2,1,0:T(8,128)S(1)}) custom-call(s32[1,6]{1,0:T(1,128)} %levels.7, s32[1]{0:T(128)S(6)} %copy.5.coefs, f32[1,4,4,4,8,8,128]{6,5,4,3,2,1,0:T(8,128)} %x.3, bf16[3,128,128]{2,1,0:T(8,128)(2,1)} %constant.4.clone.pf, f32[8,1,8,8,128]{4,3,2,1,0:T(8,128)S(1)} %get-tuple-element.9.rest_0_.own0), custom_call_target="tpu_custom_call" | custom-call | flops 300000000 | bytes 3145728 | tf_op jit(solution)/shard_map/pallas_call | solution.py:131
  5.2 1.5 %collective-permute-start.2 = (f32[8,3,8,8,128]{4,3,2,1,0:T(8,128)S(1)}, f32[8,3,8,8,128]{4,3,2,1,0:T(8,128)S(1)}, u32[]{:S(2)}, u32[]{:S(2)}) collective-permute-start(f32[8,3,8,8,128]{4,3,2,1,0:T(8,128)S(1)} %get-tuple-element.12), channel_id=1, source_target_pairs={{0,8},{8,0},{16,24},{24,16},{32,40},{40,32},{48,56},{56,48},{64,72... | collective-permute-start | bytes 2359304 | tf_op jit(solution)/shard_map/ppermute | solution.py:223
  6.6 5.9 %collective-permute-start.4 = (f32[8,1,8,8,128]{4,3,2,1,0:T(8,128)S(1)}, f32[8,1,8,8,128]{4,3,2,1,0:T(8,128)S(1)}, u32[]{:S(2)}, u32[]{:S(2)}) collective-permute-start(f32[8,1,8,8,128]{4,3,2,1,0:T(8,128)S(1)} %get-tuple-element.11), channel_id=1, source_target_pairs={{0,15},{1,8},{2,9},{3,10},{4,11},{5,12},{6,13},{7,14},{8,7},{9,0},... | collective-permute-start | bytes 786440 | tf_op jit(solution)/shard_map/ppermute | solution.py:228
  12.5 0.4 collective-permute-start.1
  12.9 0.4 collective-permute-start
  13.3 0.8 %collective-permute-done.others = s32[1,6]{1,0:T(1,128)S(1)} collective-permute-done((s32[1,6]{1,0:T(1,128)S(1)}, s32[1,6]{1,0:T(1,128)S(1)}, u32[]{:S(2)}, u32[]{:S(2)}) %collective-permute-start) | collective-permute-done | bytes 56 | tf_op jit(solution)/shard_map/ppermute | solution.py:223
  14.1 3.9 %collective-permute-done.4.next_got = f32[8,1,8,8,128]{4,3,2,1,0:T(8,128)S(1)} collective-permute-done((f32[8,1,8,8,128]{4,3,2,1,0:T(8,128)S(1)}, f32[8,1,8,8,128]{4,3,2,1,0:T(8,128)S(1)}, u32[]{:S(2)}, u32[]{:S(2)}) %collective-permute-start.4) | collective-permute-done | bytes 262176 | tf_op jit(solution)/shard_map/ppermute | solution.py:228
  18.0 5.6 %collective-permute-done.3.next_own = f32[8,1,8,8,128]{4,3,2,1,0:T(8,128)S(1)} collective-permute-done((f32[8,1,8,8,128]{4,3,2,1,0:T(8,128)S(1)}, f32[8,1,8,8,128]{4,3,2,1,0:T(8,128)S(1)}, u32[]{:S(2)}, u32[]{:S(2)}) %collective-permute-start.3) | collective-permute-done | bytes 262176 | tf_op jit(solution)/shard_map/ppermute | solution.py:228
  23.6 0.8 %combine.1 = f32[8,4,8,8,128]{4,3,2,1,0:T(8,128)S(1)} custom-call(s32[1,6]{1,0:T(1,128)S(1)} %copy-done, s32[1,6]{1,0:T(1,128)S(1)} %collective-permute-done.others, f32[8,1,8,8,128]{4,3,2,1,0:T(8,128)S(1)} %get-tuple-element.9.rest_0_.own0, f32[8,3,8,8,128]{4,3,2,1,0:T(8,128)S(1)} %get-tuple-element.10.own123, ...), custom_call_target="tpu_custom_call" | custom-call | tf_op jit(solution)/shard_map/combine/pallas_call | solution.py:172
  24.4 18.3 %all_to_all.5 = f32[8,4,8,8,128]{4,3,2,1,0:T(8,128)S(1)} all-to-all(f32[8,4,8,8,128]{4,3,2,1,0:T(8,128)S(1)} %combine.1), channel_id=1, replica_groups={{0,16,32,48,64,80,96,112},{8,24,40,56,72,88,104,120},{1,17,33,49,65,81,..., dimensions={0} | all-to-all | bytes 2097152 | tf_op jit(solution)/shard_map/all_to_all | solution.py:241
  42.7 0.1 reduce_sum.9.refs_0_
  42.8 1.9 %collective-permute-start.18 = (f32[4,8,8,128]{3,2,1,0:T(8,128)S(1)}, f32[4,8,8,128]{3,2,1,0:T(8,128)S(1)}, u32[]{:S(2)}, u32[]{:S(2)}) collective-permute-start(f32[4,8,8,128]{3,2,1,0:T(8,128)S(1)} %reduce_sum.9.refs_0_), channel_id=1, source_target_pairs={{0,112},{8,120},{16,96},{24,104},{32,80},{40,88},{48,64},{56,72},{... | collective-permute-start | bytes 393224 | tf_op jit(solution)/shard_map/ppermute | solution.py:223
  44.7 1.8 %collective-permute-start.16 = (f32[4,8,8,128]{3,2,1,0:T(8,128)S(1)}, f32[4,8,8,128]{3,2,1,0:T(8,128)S(1)}, u32[]{:S(2)}, u32[]{:S(2)}) collective-permute-start(f32[4,8,8,128]{3,2,1,0:T(8,128)S(1)} %reduce_sum.9.refs_0_), channel_id=1, source_target_pairs={{0,96},{8,104},{16,112},{24,120},{32,64},{40,72},{48,80},{56,88},{... | collective-permute-start | bytes 393224 | tf_op jit(solution)/shard_map/ppermute | solution.py:223
  46.5 3.0 %collective-permute-start.12 = (f32[4,8,8,128]{3,2,1,0:T(8,128)S(1)}, f32[4,8,8,128]{3,2,1,0:T(8,128)S(1)}, u32[]{:S(2)}, u32[]{:S(2)}) collective-permute-start(f32[4,8,8,128]{3,2,1,0:T(8,128)S(1)} %reduce_sum.9.refs_0_), channel_id=1, source_target_pairs={{0,64},{8,72},{16,80},{24,88},{32,96},{40,104},{48,112},{56,120},{... | collective-permute-start | bytes 393224 | tf_op jit(solution)/shard_map/ppermute | solution.py:223
  49.5 2.4 %collective-permute-start.8 = (f32[4,8,8,128]{3,2,1,0:T(8,128)S(1)}, f32[4,8,8,128]{3,2,1,0:T(8,128)S(1)}, u32[]{:S(2)}, u32[]{:S(2)}) collective-permute-start(f32[4,8,8,128]{3,2,1,0:T(8,128)S(1)} %reduce_sum.9.refs_0_), channel_id=1, source_target_pairs={{0,32},{8,40},{16,48},{24,56},{32,0},{40,8},{48,16},{56,24},{64,96... | collective-permute-start | bytes 393224 | tf_op jit(solution)/shard_map/ppermute | solution.py:223
  51.8 0.3 collective-permute-start.6
  52.1 0.7 %collective-permute-done.14.refs_10_ = f32[4,8,8,128]{3,2,1,0:T(8,128)S(1)} collective-permute-done((f32[4,8,8,128]{3,2,1,0:T(8,128)S(1)}, f32[4,8,8,128]{3,2,1,0:T(8,128)S(1)}, u32[]{:S(2)}, u32[]{:S(2)}) %collective-permute-start.14) | collective-permute-done | bytes 131104 | tf_op jit(solution)/shard_map/ppermute | solution.py:223
  52.8 5.8 %collective-permute-start.5 = (f32[4,8,8,128]{3,2,1,0:T(8,128)S(1)}, f32[4,8,8,128]{3,2,1,0:T(8,128)S(1)}, u32[]{:S(2)}, u32[]{:S(2)}) collective-permute-start(f32[4,8,8,128]{3,2,1,0:T(8,128)S(1)} %reduce_sum.9.refs_0_), channel_id=1, source_target_pairs={{0,8},{8,0},{16,24},{24,16},{32,40},{40,32},{48,56},{56,48},{64,72... | collective-permute-start | bytes 393224 | tf_op jit(solution)/shard_map/ppermute | solution.py:223
  58.6 1.1 %collective-permute-start.19 = (f32[4,8,8,128]{3,2,1,0:T(8,128)S(1)}, f32[4,8,8,128]{3,2,1,0:T(8,128)S(1)}, u32[]{:S(2)}, u32[]{:S(2)}) collective-permute-start(f32[4,8,8,128]{3,2,1,0:T(8,128)S(1)} %collective-permute-done.18.refs_14_), channel_id=1, source_target_pairs={{0,8},{8,0},{16,24},{24,16},{32,40},{40,32},{48,56},{56,48},{64,72... | collective-permute-start | bytes 393224 | tf_op jit(solution)/shard_map/ppermute | solution.py:223
  59.7 0.8 %collective-permute-start.17 = (f32[4,8,8,128]{3,2,1,0:T(8,128)S(1)}, f32[4,8,8,128]{3,2,1,0:T(8,128)S(1)}, u32[]{:S(2)}, u32[]{:S(2)}) collective-permute-start(f32[4,8,8,128]{3,2,1,0:T(8,128)S(1)} %collective-permute-done.16.refs_12_), channel_id=1, source_target_pairs={{0,8},{8,0},{16,24},{24,16},{32,40},{40,32},{48,56},{56,48},{64,72... | collective-permute-start | bytes 393224 | tf_op jit(solution)/shard_map/ppermute | solution.py:223
  60.5 0.9 %collective-permute-start.15 = (f32[4,8,8,128]{3,2,1,0:T(8,128)S(1)}, f32[4,8,8,128]{3,2,1,0:T(8,128)S(1)}, u32[]{:S(2)}, u32[]{:S(2)}) collective-permute-start(f32[4,8,8,128]{3,2,1,0:T(8,128)S(1)} %collective-permute-done.14.refs_10_), channel_id=1, source_target_pairs={{0,8},{8,0},{16,24},{24,16},{32,40},{40,32},{48,56},{56,48},{64,72... | collective-permute-start | bytes 393224 | tf_op jit(solution)/shard_map/ppermute | solution.py:223
  61.4 2.2 %collective-permute-start.13 = (f32[4,8,8,128]{3,2,1,0:T(8,128)S(1)}, f32[4,8,8,128]{3,2,1,0:T(8,128)S(1)}, u32[]{:S(2)}, u32[]{:S(2)}) collective-permute-start(f32[4,8,8,128]{3,2,1,0:T(8,128)S(1)} %collective-permute-done.12.refs_8_), channel_id=1, source_target_pairs={{0,8},{8,0},{16,24},{24,16},{32,40},{40,32},{48,56},{56,48},{64,72... | collective-permute-start | bytes 393224 | tf_op jit(solution)/shard_map/ppermute | solution.py:223
  63.5 0.0 collective-permute-start.11
  63.6 0.5 collective-permute-start.9
  64.1 0.1 collective-permute-start.7
  64.2 0.4 collective-permute-done.13.refs_9_
  64.5 0.4 collective-permute-done.11.refs_7_
  64.9 0.2 collective-permute-done.9.refs_5_
  65.1 0.3 collective-permute-done.7.refs_3_
  65.4 2.1 %restrict.1 = f32[4,16,8,8,128]{4,3,2,1,0:T(8,128)} custom-call(s32[1,6]{1,0:T(1,128)S(1)} %copy-done, f32[4,8,8,128]{3,2,1,0:T(8,128)S(1)} %reduce_sum.9.refs_0_, f32[4,8,8,128]{3,2,1,0:T(8,128)S(1)} %collective-permute-done.5.refs_1_, f32[4,8,8,128]{3,2,1,0:T(8,128)S(1)} %collective-permute-done.6.refs_2_, ...), custom_call_target="tpu_custom_call" | custom-call | tf_op jit(solution)/shard_map/restrict/pallas_call | solution.py:210
  (16 shorter events, 0.0 us)
Async XLA Ops:
  0.7 12.3 %copy-start = (s32[1,6]{1,0:T(1,128)S(1)}, s32[1,6]{1,0:T(1,128)}, u32[]{:S(2)}) copy-start(s32[1,6]{1,0:T(1,128)} %levels.7) | copy-start | bytes 76
  5.2 18.5 %collective-permute-start.2 = (f32[8,3,8,8,128]{4,3,2,1,0:T(8,128)S(1)}, f32[8,3,8,8,128]{4,3,2,1,0:T(8,128)S(1)}, u32[]{:S(2)}, u32[]{:S(2)}) collective-permute-start(f32[8,3,8,8,128]{4,3,2,1,0:T(8,128)S(1)} %get-tuple-element.12), channel_id=1, source_target_pairs={{0,8},{8,0},{16,24},{24,16},{32,40},{40,32},{48,56},{56,48},{64,72... | collective-permute-start | bytes 2359304 | tf_op jit(solution)/shard_map/ppermute | solution.py:223
  6.6 11.4 %collective-permute-start.4 = (f32[8,1,8,8,128]{4,3,2,1,0:T(8,128)S(1)}, f32[8,1,8,8,128]{4,3,2,1,0:T(8,128)S(1)}, u32[]{:S(2)}, u32[]{:S(2)}) collective-permute-start(f32[8,1,8,8,128]{4,3,2,1,0:T(8,128)S(1)} %get-tuple-element.11), channel_id=1, source_target_pairs={{0,15},{1,8},{2,9},{3,10},{4,11},{5,12},{6,13},{7,14},{8,7},{9,0},... | collective-permute-start | bytes 786440 | tf_op jit(solution)/shard_map/ppermute | solution.py:228
  12.5 5.5 %collective-permute-start.1 = (f32[8,1,8,8,128]{4,3,2,1,0:T(8,128)S(1)}, f32[8,1,8,8,128]{4,3,2,1,0:T(8,128)S(1)}, u32[]{:S(2)}, u32[]{:S(2)}) collective-permute-start(f32[8,1,8,8,128]{4,3,2,1,0:T(8,128)S(1)} %get-tuple-element.11), channel_id=1, source_target_pairs={{0,8},{8,0},{16,24},{24,16},{32,40},{40,32},{48,56},{56,48},{64,72... | collective-permute-start | bytes 786440 | tf_op jit(solution)/shard_map/ppermute | solution.py:223
  12.9 10.7 %collective-permute-start.3 = (f32[8,1,8,8,128]{4,3,2,1,0:T(8,128)S(1)}, f32[8,1,8,8,128]{4,3,2,1,0:T(8,128)S(1)}, u32[]{:S(2)}, u32[]{:S(2)}) collective-permute-start(f32[8,1,8,8,128]{4,3,2,1,0:T(8,128)S(1)} %get-tuple-element.9.rest_0_.own0), channel_id=1, source_target_pairs={{0,7},{1,0},{2,1},{3,2},{4,3},{5,4},{6,5},{7,6},{8,15},{9,8},{10,9... | collective-permute-start | bytes 786440 | tf_op jit(solution)/shard_map/ppermute | solution.py:228
  12.9 1.2 %collective-permute-start = (s32[1,6]{1,0:T(1,128)S(1)}, s32[1,6]{1,0:T(1,128)S(1)}, u32[]{:S(2)}, u32[]{:S(2)}) collective-permute-start(s32[1,6]{1,0:T(1,128)S(1)} %copy-done), channel_id=1, source_target_pairs={{0,8},{8,0},{16,24},{24,16},{32,40},{40,32},{48,56},{56,48},{64,72... | collective-permute-start | bytes 80 | tf_op jit(solution)/shard_map/ppermute | solution.py:223
  42.8 6.6 %collective-permute-start.18 = (f32[4,8,8,128]{3,2,1,0:T(8,128)S(1)}, f32[4,8,8,128]{3,2,1,0:T(8,128)S(1)}, u32[]{:S(2)}, u32[]{:S(2)}) collective-permute-start(f32[4,8,8,128]{3,2,1,0:T(8,128)S(1)} %reduce_sum.9.refs_0_), channel_id=1, source_target_pairs={{0,112},{8,120},{16,96},{24,104},{32,80},{40,88},{48,64},{56,72},{... | collective-permute-start | bytes 393224 | tf_op jit(solution)/shard_map/ppermute | solution.py:223
  44.7 7.1 %collective-permute-start.16 = (f32[4,8,8,128]{3,2,1,0:T(8,128)S(1)}, f32[4,8,8,128]{3,2,1,0:T(8,128)S(1)}, u32[]{:S(2)}, u32[]{:S(2)}) collective-permute-start(f32[4,8,8,128]{3,2,1,0:T(8,128)S(1)} %reduce_sum.9.refs_0_), channel_id=1, source_target_pairs={{0,96},{8,104},{16,112},{24,120},{32,64},{40,72},{48,80},{56,88},{... | collective-permute-start | bytes 393224 | tf_op jit(solution)/shard_map/ppermute | solution.py:223
  46.5 6.3 %collective-permute-start.14 = (f32[4,8,8,128]{3,2,1,0:T(8,128)S(1)}, f32[4,8,8,128]{3,2,1,0:T(8,128)S(1)}, u32[]{:S(2)}, u32[]{:S(2)}) collective-permute-start(f32[4,8,8,128]{3,2,1,0:T(8,128)S(1)} %reduce_sum.9.refs_0_), channel_id=1, source_target_pairs={{0,80},{8,88},{16,64},{24,72},{32,112},{40,120},{48,96},{56,104},{... | collective-permute-start | bytes 393224 | tf_op jit(solution)/shard_map/ppermute | solution.py:223
  46.5 12.1 %collective-permute-start.12 = (f32[4,8,8,128]{3,2,1,0:T(8,128)S(1)}, f32[4,8,8,128]{3,2,1,0:T(8,128)S(1)}, u32[]{:S(2)}, u32[]{:S(2)}) collective-permute-start(f32[4,8,8,128]{3,2,1,0:T(8,128)S(1)} %reduce_sum.9.refs_0_), channel_id=1, source_target_pairs={{0,64},{8,72},{16,80},{24,88},{32,96},{40,104},{48,112},{56,120},{... | collective-permute-start | bytes 393224 | tf_op jit(solution)/shard_map/ppermute | solution.py:223
  49.4 10.2 %collective-permute-start.10 = (f32[4,8,8,128]{3,2,1,0:T(8,128)S(1)}, f32[4,8,8,128]{3,2,1,0:T(8,128)S(1)}, u32[]{:S(2)}, u32[]{:S(2)}) collective-permute-start(f32[4,8,8,128]{3,2,1,0:T(8,128)S(1)} %reduce_sum.9.refs_0_), channel_id=1, source_target_pairs={{0,48},{8,56},{16,32},{24,40},{32,16},{40,24},{48,0},{56,8},{64,11... | collective-permute-start | bytes 393224 | tf_op jit(solution)/shard_map/ppermute | solution.py:223
  49.5 11.0 %collective-permute-start.8 = (f32[4,8,8,128]{3,2,1,0:T(8,128)S(1)}, f32[4,8,8,128]{3,2,1,0:T(8,128)S(1)}, u32[]{:S(2)}, u32[]{:S(2)}) collective-permute-start(f32[4,8,8,128]{3,2,1,0:T(8,128)S(1)} %reduce_sum.9.refs_0_), channel_id=1, source_target_pairs={{0,32},{8,40},{16,48},{24,56},{32,0},{40,8},{48,16},{56,24},{64,96... | collective-permute-start | bytes 393224 | tf_op jit(solution)/shard_map/ppermute | solution.py:223
  51.8 9.5 %collective-permute-start.6 = (f32[4,8,8,128]{3,2,1,0:T(8,128)S(1)}, f32[4,8,8,128]{3,2,1,0:T(8,128)S(1)}, u32[]{:S(2)}, u32[]{:S(2)}) collective-permute-start(f32[4,8,8,128]{3,2,1,0:T(8,128)S(1)} %reduce_sum.9.refs_0_), channel_id=1, source_target_pairs={{0,16},{8,24},{16,0},{24,8},{32,48},{40,56},{48,32},{56,40},{64,80... | collective-permute-start | bytes 393224 | tf_op jit(solution)/shard_map/ppermute | solution.py:223
  52.8 10.7 %collective-permute-start.5 = (f32[4,8,8,128]{3,2,1,0:T(8,128)S(1)}, f32[4,8,8,128]{3,2,1,0:T(8,128)S(1)}, u32[]{:S(2)}, u32[]{:S(2)}) collective-permute-start(f32[4,8,8,128]{3,2,1,0:T(8,128)S(1)} %reduce_sum.9.refs_0_), channel_id=1, source_target_pairs={{0,8},{8,0},{16,24},{24,16},{32,40},{40,32},{48,56},{56,48},{64,72... | collective-permute-start | bytes 393224 | tf_op jit(solution)/shard_map/ppermute | solution.py:223
  58.6 5.0 %collective-permute-start.19 = (f32[4,8,8,128]{3,2,1,0:T(8,128)S(1)}, f32[4,8,8,128]{3,2,1,0:T(8,128)S(1)}, u32[]{:S(2)}, u32[]{:S(2)}) collective-permute-start(f32[4,8,8,128]{3,2,1,0:T(8,128)S(1)} %collective-permute-done.18.refs_14_), channel_id=1, source_target_pairs={{0,8},{8,0},{16,24},{24,16},{32,40},{40,32},{48,56},{56,48},{64,72... | collective-permute-start | bytes 393224 | tf_op jit(solution)/shard_map/ppermute | solution.py:223
  59.7 4.4 %collective-permute-start.17 = (f32[4,8,8,128]{3,2,1,0:T(8,128)S(1)}, f32[4,8,8,128]{3,2,1,0:T(8,128)S(1)}, u32[]{:S(2)}, u32[]{:S(2)}) collective-permute-start(f32[4,8,8,128]{3,2,1,0:T(8,128)S(1)} %collective-permute-done.16.refs_12_), channel_id=1, source_target_pairs={{0,8},{8,0},{16,24},{24,16},{32,40},{40,32},{48,56},{56,48},{64,72... | collective-permute-start | bytes 393224 | tf_op jit(solution)/shard_map/ppermute | solution.py:223
  60.5 3.7 %collective-permute-start.15 = (f32[4,8,8,128]{3,2,1,0:T(8,128)S(1)}, f32[4,8,8,128]{3,2,1,0:T(8,128)S(1)}, u32[]{:S(2)}, u32[]{:S(2)}) collective-permute-start(f32[4,8,8,128]{3,2,1,0:T(8,128)S(1)} %collective-permute-done.14.refs_10_), channel_id=1, source_target_pairs={{0,8},{8,0},{16,24},{24,16},{32,40},{40,32},{48,56},{56,48},{64,72... | collective-permute-start | bytes 393224 | tf_op jit(solution)/shard_map/ppermute | solution.py:223
  61.4 3.2 %collective-permute-start.13 = (f32[4,8,8,128]{3,2,1,0:T(8,128)S(1)}, f32[4,8,8,128]{3,2,1,0:T(8,128)S(1)}, u32[]{:S(2)}, u32[]{:S(2)}) collective-permute-start(f32[4,8,8,128]{3,2,1,0:T(8,128)S(1)} %collective-permute-done.12.refs_8_), channel_id=1, source_target_pairs={{0,8},{8,0},{16,24},{24,16},{32,40},{40,32},{48,56},{56,48},{64,72... | collective-permute-start | bytes 393224 | tf_op jit(solution)/shard_map/ppermute | solution.py:223
  63.5 1.3 %collective-permute-start.11 = (f32[4,8,8,128]{3,2,1,0:T(8,128)S(1)}, f32[4,8,8,128]{3,2,1,0:T(8,128)S(1)}, u32[]{:S(2)}, u32[]{:S(2)}) collective-permute-start(f32[4,8,8,128]{3,2,1,0:T(8,128)S(1)} %collective-permute-done.10.refs_6_), channel_id=1, source_target_pairs={{0,8},{8,0},{16,24},{24,16},{32,40},{40,32},{48,56},{56,48},{64,72... | collective-permute-start | bytes 393224 | tf_op jit(solution)/shard_map/ppermute | solution.py:223
  63.6 1.5 %collective-permute-start.9 = (f32[4,8,8,128]{3,2,1,0:T(8,128)S(1)}, f32[4,8,8,128]{3,2,1,0:T(8,128)S(1)}, u32[]{:S(2)}, u32[]{:S(2)}) collective-permute-start(f32[4,8,8,128]{3,2,1,0:T(8,128)S(1)} %collective-permute-done.8.refs_4_), channel_id=1, source_target_pairs={{0,8},{8,0},{16,24},{24,16},{32,40},{40,32},{48,56},{56,48},{64,72... | collective-permute-start | bytes 393224 | tf_op jit(solution)/shard_map/ppermute | solution.py:223
  64.1 1.3 %collective-permute-start.7 = (f32[4,8,8,128]{3,2,1,0:T(8,128)S(1)}, f32[4,8,8,128]{3,2,1,0:T(8,128)S(1)}, u32[]{:S(2)}, u32[]{:S(2)}) collective-permute-start(f32[4,8,8,128]{3,2,1,0:T(8,128)S(1)} %collective-permute-done.6.refs_2_), channel_id=1, source_target_pairs={{0,8},{8,0},{16,24},{24,16},{32,40},{40,32},{48,56},{56,48},{64,72... | collective-permute-start | bytes 393224 | tf_op jit(solution)/shard_map/ppermute | solution.py:223
where the time goes:
time: 67.7 us; the launch traced here: 67.5 us
  starting transfers between devices  28.8 us (43%)
  blocking collectives  18.3 us (27%)
  waiting for transfers between devices  12.3 us (18%)
  Pallas kernels  7.34 us (11%)
  between operations  0.71 us (1%)
    ppermute x18, starting transfers between devices, swap(): return lax.ppermute(x, 'grid', [(i, i ^ bits) for i in range(16)])  22.9 us
    all_to_all x1, blocking collectives, whole(): lax.all_to_all(parts, 'grid', split_axis=0, concat_axis=0, axis_index_gro...  18.3 us
    ppermute x2, waiting for transfers between devices, to_previous(): return lax.ppermute(x, ('grid', 'dom'), pairs)  9.48 us
    ppermute x2, starting transfers between devices, to_previous(): return lax.ppermute(x, ('grid', 'dom'), pairs)  5.88 us
    pallas_call x2, Pallas kernels, interp_rows(): pl.pallas_call(interp_kernel, grid=(count,), in_specs=[smem, smem, pl.Blo...  4.47 us
    ppermute x18, waiting for transfers between devices, swap(): return lax.ppermute(x, 'grid', [(i, i ^ bits) for i in range(16)])  2.81 us
    pallas_call x1, Pallas kernels, restrict(): pl.pallas_call(restrict_kernel, in_specs=[pl.BlockSpec(memory_space=pltpu...  2.08 us
  transfers between devices with their start and end apart: 20, of which 8 were waited for; matrix products, arithmetic and copies ran while one was open for 0% of the time, Pallas kernels for 0%

commit v1 on v0

--- a/solution.py
+++ b/solution.py
@@ -228,6 +228,9 @@
     return lax.ppermute(x, ("grid", "dom"), pairs)
 
 
+GATHER = ((2, 0), (8, 0), (4, 0), (12, 0), (4, 2), (12, 2), (2, 8))
+
+
 def whole(values, levels, coefficients):
     matrices = jnp.asarray(interp_tables(7).transpose(0, 2, 1), dtype=jnp.bfloat16)
     others = swap(levels, 1)
@@ -241,8 +244,8 @@
     arrived = lax.all_to_all(parts, "grid", split_axis=0, concat_axis=0, axis_index_groups=groups, tiled=True)
     share = arrived.sum(axis=0)
     pieces = {0: share}
-    for bits in (4, 12, 2, 6, 14, 8, 10):
-        pieces[bits] = swap(share, bits)
+    for bits, first in GATHER:
+        pieces[bits ^ first] = swap(pieces[first], bits)
     for bits in list(pieces):
         pieces[bits + 1] = swap(pieces[bits], 1)
     return restrict(levels, [pieces[slot] for slot in range(16)])

time: 67.7 us -> 65.2 us (0.963)
  starting transfers between devices: 28.8 us -> 24.4 us
  waiting for transfers between devices: 12.3 us -> 14.1 us
    ppermute x18, starting transfers between devices: 22.9 us -> 18.5 us  [swap(): return lax.ppermute(x, 'grid', [(i, i ^ bits) for i in range(16)])]
    ppermute x18, waiting for transfers between devices: 2.81 us -> 4.59 us  [swap(): return lax.ppermute(x, 'grid', [(i, i ^ bits) for i in range(16)])]
  transfers between devices with their start and end apart: 20 -> 20, of which waited for: 8 -> 7; matrix products, arithmetic and copies ran while one was open for 0% -> 0% of each run, Pallas kernels for 0% -> 0%
where the time goes in v1:
time: 65.2 us; the launch traced here: 64.9 us
  starting transfers between devices  24.4 us (37%)
  blocking collectives  18.3 us (28%)
  waiting for transfers between devices  14.1 us (22%)
  Pallas kernels  7.34 us (11%)
  between operations  0.71 us (1%)
    ppermute x18, starting transfers between devices, swap(): return lax.ppermute(x, 'grid', [(i, i ^ bits) for i in range(16)])  18.5 us
    all_to_all x1, blocking collectives, whole(): lax.all_to_all(parts, 'grid', split_axis=0, concat_axis=0, axis_index_gro...  18.3 us
    ppermute x2, waiting for transfers between devices, to_previous(): return lax.ppermute(x, ('grid', 'dom'), pairs)  9.48 us
    ppermute x2, starting transfers between devices, to_previous(): return lax.ppermute(x, ('grid', 'dom'), pairs)  5.88 us
    ppermute x18, waiting for transfers between devices, swap(): return lax.ppermute(x, 'grid', [(i, i ^ bits) for i in range(16)])  4.59 us
    pallas_call x2, Pallas kernels, interp_rows(): pl.pallas_call(interp_kernel, grid=(count,), in_specs=[smem, smem, pl.Blo...  4.47 us
    pallas_call x1, Pallas kernels, restrict(): pl.pallas_call(restrict_kernel, in_specs=[pl.BlockSpec(memory_space=pltpu...  2.08 us
  transfers between devices with their start and end apart: 20, of which 7 were waited for; matrix products, arithmetic and copies ran while one was open for 0% of the time, Pallas kernels for 0%

profile of v1, /device:TPU:1, one launch (start us, length us, event | category | flops | bytes accessed | tf_op | source)
XLA Modules:
  0.0 64.9 jit_solution(13611755843771223608)
XLA Ops:
  0.7 0.0 copy-start
  0.7 1.4 %shard_map.46 = (f32[8,1,8,8,128]{4,3,2,1,0:T(8,128)S(1)}, f32[8,1,8,8,128]{4,3,2,1,0:T(8,128)S(1)}) custom-call(s32[1,6]{1,0:T(1,128)} %levels.7, s32[1]{0:T(128)S(6)} %copy.5.coefs, f32[1,4,4,4,8,8,128]{6,5,4,3,2,1,0:T(8,128)} %x.3, bf16[3,128,128]{2,1,0:T(8,128)(2,1)} %constant.4.clone.pf), custom_call_target="tpu_custom_call" | custom-call | flops 100000000 | bytes 1048576 | tf_op jit(solution)/shard_map/pallas_call | solution.py:131
  2.1 3.0 %shard_map.47 = (f32[8,3,8,8,128]{4,3,2,1,0:T(8,128)S(1)}, f32[8,3,8,8,128]{4,3,2,1,0:T(8,128)S(1)}) custom-call(s32[1,6]{1,0:T(1,128)} %levels.7, s32[1]{0:T(128)S(6)} %copy.5.coefs, f32[1,4,4,4,8,8,128]{6,5,4,3,2,1,0:T(8,128)} %x.3, bf16[3,128,128]{2,1,0:T(8,128)(2,1)} %constant.4.clone.pf, f32[8,1,8,8,128]{4,3,2,1,0:T(8,128)S(1)} %get-tuple-element.9.rest_0_.own0), custom_call_target="tpu_custom_call" | custom-call | flops 300000000 | bytes 3145728 | tf_op jit(solution)/shard_map/pallas_call | solution.py:131
  5.2 1.5 %collective-permute-start.2 = (f32[8,3,8,8,128]{4,3,2,1,0:T(8,128)S(1)}, f32[8,3,8,8,128]{4,3,2,1,0:T(8,128)S(1)}, u32[]{:S(2)}, u32[]{:S(2)}) collective-permute-start(f32[8,3,8,8,128]{4,3,2,1,0:T(8,128)S(1)} %get-tuple-element.12), channel_id=1, source_target_pairs={{0,8},{8,0},{16,24},{24,16},{32,40},{40,32},{48,56},{56,48},{64,72... | collective-permute-start | bytes 2359304 | tf_op jit(solution)/shard_map/ppermute | solution.py:223
  6.6 5.9 %collective-permute-start.4 = (f32[8,1,8,8,128]{4,3,2,1,0:T(8,128)S(1)}, f32[8,1,8,8,128]{4,3,2,1,0:T(8,128)S(1)}, u32[]{:S(2)}, u32[]{:S(2)}) collective-permute-start(f32[8,1,8,8,128]{4,3,2,1,0:T(8,128)S(1)} %get-tuple-element.11), channel_id=1, source_target_pairs={{0,15},{1,8},{2,9},{3,10},{4,11},{5,12},{6,13},{7,14},{8,7},{9,0},... | collective-permute-start | bytes 786440 | tf_op jit(solution)/shard_map/ppermute | solution.py:228
  12.5 0.4 collective-permute-start.1
  12.9 0.4 collective-permute-start
  13.3 0.8 %collective-permute-done.others = s32[1,6]{1,0:T(1,128)S(1)} collective-permute-done((s32[1,6]{1,0:T(1,128)S(1)}, s32[1,6]{1,0:T(1,128)S(1)}, u32[]{:S(2)}, u32[]{:S(2)}) %collective-permute-start) | collective-permute-done | bytes 56 | tf_op jit(solution)/shard_map/ppermute | solution.py:223
  14.1 3.9 %collective-permute-done.4.next_got = f32[8,1,8,8,128]{4,3,2,1,0:T(8,128)S(1)} collective-permute-done((f32[8,1,8,8,128]{4,3,2,1,0:T(8,128)S(1)}, f32[8,1,8,8,128]{4,3,2,1,0:T(8,128)S(1)}, u32[]{:S(2)}, u32[]{:S(2)}) %collective-permute-start.4) | collective-permute-done | bytes 262176 | tf_op jit(solution)/shard_map/ppermute | solution.py:228
  18.0 5.6 %collective-permute-done.3.next_own = f32[8,1,8,8,128]{4,3,2,1,0:T(8,128)S(1)} collective-permute-done((f32[8,1,8,8,128]{4,3,2,1,0:T(8,128)S(1)}, f32[8,1,8,8,128]{4,3,2,1,0:T(8,128)S(1)}, u32[]{:S(2)}, u32[]{:S(2)}) %collective-permute-start.3) | collective-permute-done | bytes 262176 | tf_op jit(solution)/shard_map/ppermute | solution.py:228
  23.6 0.8 %combine.1 = f32[8,4,8,8,128]{4,3,2,1,0:T(8,128)S(1)} custom-call(s32[1,6]{1,0:T(1,128)S(1)} %copy-done, s32[1,6]{1,0:T(1,128)S(1)} %collective-permute-done.others, f32[8,1,8,8,128]{4,3,2,1,0:T(8,128)S(1)} %get-tuple-element.9.rest_0_.own0, f32[8,3,8,8,128]{4,3,2,1,0:T(8,128)S(1)} %get-tuple-element.10.own123, ...), custom_call_target="tpu_custom_call" | custom-call | tf_op jit(solution)/shard_map/combine/pallas_call | solution.py:172
  24.4 18.3 %all_to_all.5 = f32[8,4,8,8,128]{4,3,2,1,0:T(8,128)S(1)} all-to-all(f32[8,4,8,8,128]{4,3,2,1,0:T(8,128)S(1)} %combine.1), channel_id=1, replica_groups={{0,16,32,48,64,80,96,112},{8,24,40,56,72,88,104,120},{1,17,33,49,65,81,..., dimensions={0} | all-to-all | bytes 2097152 | tf_op jit(solution)/shard_map/all_to_all | solution.py:244
  42.7 0.1 reduce_sum.9.refs_0_
  42.8 1.0 %collective-permute-start.16 = (f32[4,8,8,128]{3,2,1,0:T(8,128)S(1)}, f32[4,8,8,128]{3,2,1,0:T(8,128)S(1)}, u32[]{:S(2)}, u32[]{:S(2)}) collective-permute-start(f32[4,8,8,128]{3,2,1,0:T(8,128)S(1)} %reduce_sum.9.refs_0_), channel_id=1, source_target_pairs={{0,96},{8,104},{16,112},{24,120},{32,64},{40,72},{48,80},{56,88},{... | collective-permute-start | bytes 393224 | tf_op jit(solution)/shard_map/ppermute | solution.py:223
  43.8 1.2 %collective-permute-start.12 = (f32[4,8,8,128]{3,2,1,0:T(8,128)S(1)}, f32[4,8,8,128]{3,2,1,0:T(8,128)S(1)}, u32[]{:S(2)}, u32[]{:S(2)}) collective-permute-start(f32[4,8,8,128]{3,2,1,0:T(8,128)S(1)} %reduce_sum.9.refs_0_), channel_id=1, source_target_pairs={{0,64},{8,72},{16,80},{24,88},{32,96},{40,104},{48,112},{56,120},{... | collective-permute-start | bytes 393224 | tf_op jit(solution)/shard_map/ppermute | solution.py:223
  45.0 1.2 %collective-permute-start.8 = (f32[4,8,8,128]{3,2,1,0:T(8,128)S(1)}, f32[4,8,8,128]{3,2,1,0:T(8,128)S(1)}, u32[]{:S(2)}, u32[]{:S(2)}) collective-permute-start(f32[4,8,8,128]{3,2,1,0:T(8,128)S(1)} %reduce_sum.9.refs_0_), channel_id=1, source_target_pairs={{0,32},{8,40},{16,48},{24,56},{32,0},{40,8},{48,16},{56,24},{64,96... | collective-permute-start | bytes 393224 | tf_op jit(solution)/shard_map/ppermute | solution.py:223
  46.2 1.2 %collective-permute-start.6 = (f32[4,8,8,128]{3,2,1,0:T(8,128)S(1)}, f32[4,8,8,128]{3,2,1,0:T(8,128)S(1)}, u32[]{:S(2)}, u32[]{:S(2)}) collective-permute-start(f32[4,8,8,128]{3,2,1,0:T(8,128)S(1)} %reduce_sum.9.refs_0_), channel_id=1, source_target_pairs={{0,16},{8,24},{16,0},{24,8},{32,48},{40,56},{48,32},{56,40},{64,80... | collective-permute-start | bytes 393224 | tf_op jit(solution)/shard_map/ppermute | solution.py:223
  47.3 3.3 %collective-permute-start.5 = (f32[4,8,8,128]{3,2,1,0:T(8,128)S(1)}, f32[4,8,8,128]{3,2,1,0:T(8,128)S(1)}, u32[]{:S(2)}, u32[]{:S(2)}) collective-permute-start(f32[4,8,8,128]{3,2,1,0:T(8,128)S(1)} %reduce_sum.9.refs_0_), channel_id=1, source_target_pairs={{0,8},{8,0},{16,24},{24,16},{32,40},{40,32},{48,56},{56,48},{64,72... | collective-permute-start | bytes 393224 | tf_op jit(solution)/shard_map/ppermute | solution.py:223
  50.6 0.9 %collective-permute-start.17 = (f32[4,8,8,128]{3,2,1,0:T(8,128)S(1)}, f32[4,8,8,128]{3,2,1,0:T(8,128)S(1)}, u32[]{:S(2)}, u32[]{:S(2)}) collective-permute-start(f32[4,8,8,128]{3,2,1,0:T(8,128)S(1)} %collective-permute-done.16.refs_12_), channel_id=1, source_target_pairs={{0,8},{8,0},{16,24},{24,16},{32,40},{40,32},{48,56},{56,48},{64,72... | collective-permute-start | bytes 393224 | tf_op jit(solution)/shard_map/ppermute | solution.py:223
  51.5 2.5 %collective-permute-start.14 = (f32[4,8,8,128]{3,2,1,0:T(8,128)S(1)}, f32[4,8,8,128]{3,2,1,0:T(8,128)S(1)}, u32[]{:S(2)}, u32[]{:S(2)}) collective-permute-start(f32[4,8,8,128]{3,2,1,0:T(8,128)S(1)} %collective-permute-done.12.refs_8_), channel_id=1, source_target_pairs={{0,16},{8,24},{16,0},{24,8},{32,48},{40,56},{48,32},{56,40},{64,80... | collective-permute-start | bytes 393224 | tf_op jit(solution)/shard_map/ppermute | solution.py:223
  54.0 0.3 collective-permute-start.13
  54.3 1.6 %collective-permute-start.18 = (f32[4,8,8,128]{3,2,1,0:T(8,128)S(1)}, f32[4,8,8,128]{3,2,1,0:T(8,128)S(1)}, u32[]{:S(2)}, u32[]{:S(2)}) collective-permute-start(f32[4,8,8,128]{3,2,1,0:T(8,128)S(1)} %collective-permute-done.6.refs_2_), channel_id=1, source_target_pairs={{0,96},{8,104},{16,112},{24,120},{32,64},{40,72},{48,80},{56,88},{... | collective-permute-start | bytes 393224 | tf_op jit(solution)/shard_map/ppermute | solution.py:223
  55.9 0.4 collective-permute-start.7
  56.4 0.9 %collective-permute-done.14.refs_10_ = f32[4,8,8,128]{3,2,1,0:T(8,128)S(1)} collective-permute-done((f32[4,8,8,128]{3,2,1,0:T(8,128)S(1)}, f32[4,8,8,128]{3,2,1,0:T(8,128)S(1)}, u32[]{:S(2)}, u32[]{:S(2)}) %collective-permute-start.14) | collective-permute-done | bytes 131104 | tf_op jit(solution)/shard_map/ppermute | solution.py:223
  57.3 1.2 %collective-permute-start.9 = (f32[4,8,8,128]{3,2,1,0:T(8,128)S(1)}, f32[4,8,8,128]{3,2,1,0:T(8,128)S(1)}, u32[]{:S(2)}, u32[]{:S(2)}) collective-permute-start(f32[4,8,8,128]{3,2,1,0:T(8,128)S(1)} %collective-permute-done.8.refs_4_), channel_id=1, source_target_pairs={{0,8},{8,0},{16,24},{24,16},{32,40},{40,32},{48,56},{56,48},{64,72... | collective-permute-start | bytes 393224 | tf_op jit(solution)/shard_map/ppermute | solution.py:223
  58.5 0.0 collective-permute-start.15
  58.5 1.9 %collective-permute-done.18.refs_14_ = f32[4,8,8,128]{3,2,1,0:T(8,128)S(1)} collective-permute-done((f32[4,8,8,128]{3,2,1,0:T(8,128)S(1)}, f32[4,8,8,128]{3,2,1,0:T(8,128)S(1)}, u32[]{:S(2)}, u32[]{:S(2)}) %collective-permute-start.18) | collective-permute-done | bytes 131104 | tf_op jit(solution)/shard_map/ppermute | solution.py:223
  60.3 1.1 %collective-permute-start.19 = (f32[4,8,8,128]{3,2,1,0:T(8,128)S(1)}, f32[4,8,8,128]{3,2,1,0:T(8,128)S(1)}, u32[]{:S(2)}, u32[]{:S(2)}) collective-permute-start(f32[4,8,8,128]{3,2,1,0:T(8,128)S(1)} %collective-permute-done.18.refs_14_), channel_id=1, source_target_pairs={{0,8},{8,0},{16,24},{24,16},{32,40},{40,32},{48,56},{56,48},{64,72... | collective-permute-start | bytes 393224 | tf_op jit(solution)/shard_map/ppermute | solution.py:223
  61.4 0.4 collective-permute-start.11
  61.9 0.6 collective-permute-done.19.refs_15_
  62.4 0.4 collective-permute-done.11.refs_7_
  62.8 2.1 %restrict.1 = f32[4,16,8,8,128]{4,3,2,1,0:T(8,128)} custom-call(s32[1,6]{1,0:T(1,128)S(1)} %copy-done, f32[4,8,8,128]{3,2,1,0:T(8,128)S(1)} %reduce_sum.9.refs_0_, f32[4,8,8,128]{3,2,1,0:T(8,128)S(1)} %collective-permute-done.5.refs_1_, f32[4,8,8,128]{3,2,1,0:T(8,128)S(1)} %collective-permute-done.6.refs_2_, ...), custom_call_target="tpu_custom_call" | custom-call | tf_op jit(solution)/shard_map/restrict/pallas_call | solution.py:210
  (16 shorter events, 0.0 us)
Async XLA Ops:
  0.7 12.3 %copy-start = (s32[1,6]{1,0:T(1,128)S(1)}, s32[1,6]{1,0:T(1,128)}, u32[]{:S(2)}) copy-start(s32[1,6]{1,0:T(1,128)} %levels.7) | copy-start | bytes 76
  5.2 18.5 %collective-permute-start.2 = (f32[8,3,8,8,128]{4,3,2,1,0:T(8,128)S(1)}, f32[8,3,8,8,128]{4,3,2,1,0:T(8,128)S(1)}, u32[]{:S(2)}, u32[]{:S(2)}) collective-permute-start(f32[8,3,8,8,128]{4,3,2,1,0:T(8,128)S(1)} %get-tuple-element.12), channel_id=1, source_target_pairs={{0,8},{8,0},{16,24},{24,16},{32,40},{40,32},{48,56},{56,48},{64,72... | collective-permute-start | bytes 2359304 | tf_op jit(solution)/shard_map/ppermute | solution.py:223
  6.6 11.4 %collective-permute-start.4 = (f32[8,1,8,8,128]{4,3,2,1,0:T(8,128)S(1)}, f32[8,1,8,8,128]{4,3,2,1,0:T(8,128)S(1)}, u32[]{:S(2)}, u32[]{:S(2)}) collective-permute-start(f32[8,1,8,8,128]{4,3,2,1,0:T(8,128)S(1)} %get-tuple-element.11), channel_id=1, source_target_pairs={{0,15},{1,8},{2,9},{3,10},{4,11},{5,12},{6,13},{7,14},{8,7},{9,0},... | collective-permute-start | bytes 786440 | tf_op jit(solution)/shard_map/ppermute | solution.py:228
  12.5 5.5 %collective-permute-start.1 = (f32[8,1,8,8,128]{4,3,2,1,0:T(8,128)S(1)}, f32[8,1,8,8,128]{4,3,2,1,0:T(8,128)S(1)}, u32[]{:S(2)}, u32[]{:S(2)}) collective-permute-start(f32[8,1,8,8,128]{4,3,2,1,0:T(8,128)S(1)} %get-tuple-element.11), channel_id=1, source_target_pairs={{0,8},{8,0},{16,24},{24,16},{32,40},{40,32},{48,56},{56,48},{64,72... | collective-permute-start | bytes 786440 | tf_op jit(solution)/shard_map/ppermute | solution.py:223
  12.9 10.7 %collective-permute-start.3 = (f32[8,1,8,8,128]{4,3,2,1,0:T(8,128)S(1)}, f32[8,1,8,8,128]{4,3,2,1,0:T(8,128)S(1)}, u32[]{:S(2)}, u32[]{:S(2)}) collective-permute-start(f32[8,1,8,8,128]{4,3,2,1,0:T(8,128)S(1)} %get-tuple-element.9.rest_0_.own0), channel_id=1, source_target_pairs={{0,7},{1,0},{2,1},{3,2},{4,3},{5,4},{6,5},{7,6},{8,15},{9,8},{10,9... | collective-permute-start | bytes 786440 | tf_op jit(solution)/shard_map/ppermute | solution.py:228
  12.9 1.2 %collective-permute-start = (s32[1,6]{1,0:T(1,128)S(1)}, s32[1,6]{1,0:T(1,128)S(1)}, u32[]{:S(2)}, u32[]{:S(2)}) collective-permute-start(s32[1,6]{1,0:T(1,128)S(1)} %copy-done), channel_id=1, source_target_pairs={{0,8},{8,0},{16,24},{24,16},{32,40},{40,32},{48,56},{56,48},{64,72... | collective-permute-start | bytes 80 | tf_op jit(solution)/shard_map/ppermute | solution.py:223
  42.8 7.8 %collective-permute-start.16 = (f32[4,8,8,128]{3,2,1,0:T(8,128)S(1)}, f32[4,8,8,128]{3,2,1,0:T(8,128)S(1)}, u32[]{:S(2)}, u32[]{:S(2)}) collective-permute-start(f32[4,8,8,128]{3,2,1,0:T(8,128)S(1)} %reduce_sum.9.refs_0_), channel_id=1, source_target_pairs={{0,96},{8,104},{16,112},{24,120},{32,64},{40,72},{48,80},{56,88},{... | collective-permute-start | bytes 393224 | tf_op jit(solution)/shard_map/ppermute | solution.py:223
  43.8 7.7 %collective-permute-start.12 = (f32[4,8,8,128]{3,2,1,0:T(8,128)S(1)}, f32[4,8,8,128]{3,2,1,0:T(8,128)S(1)}, u32[]{:S(2)}, u32[]{:S(2)}) collective-permute-start(f32[4,8,8,128]{3,2,1,0:T(8,128)S(1)} %reduce_sum.9.refs_0_), channel_id=1, source_target_pairs={{0,64},{8,72},{16,80},{24,88},{32,96},{40,104},{48,112},{56,120},{... | collective-permute-start | bytes 393224 | tf_op jit(solution)/shard_map/ppermute | solution.py:223
  45.0 9.1 %collective-permute-start.8 = (f32[4,8,8,128]{3,2,1,0:T(8,128)S(1)}, f32[4,8,8,128]{3,2,1,0:T(8,128)S(1)}, u32[]{:S(2)}, u32[]{:S(2)}) collective-permute-start(f32[4,8,8,128]{3,2,1,0:T(8,128)S(1)} %reduce_sum.9.refs_0_), channel_id=1, source_target_pairs={{0,32},{8,40},{16,48},{24,56},{32,0},{40,8},{48,16},{56,24},{64,96... | collective-permute-start | bytes 393224 | tf_op jit(solution)/shard_map/ppermute | solution.py:223
  46.2 8.2 %collective-permute-start.6 = (f32[4,8,8,128]{3,2,1,0:T(8,128)S(1)}, f32[4,8,8,128]{3,2,1,0:T(8,128)S(1)}, u32[]{:S(2)}, u32[]{:S(2)}) collective-permute-start(f32[4,8,8,128]{3,2,1,0:T(8,128)S(1)} %reduce_sum.9.refs_0_), channel_id=1, source_target_pairs={{0,16},{8,24},{16,0},{24,8},{32,48},{40,56},{48,32},{56,40},{64,80... | collective-permute-start | bytes 393224 | tf_op jit(solution)/shard_map/ppermute | solution.py:223
  47.3 8.6 %collective-permute-start.5 = (f32[4,8,8,128]{3,2,1,0:T(8,128)S(1)}, f32[4,8,8,128]{3,2,1,0:T(8,128)S(1)}, u32[]{:S(2)}, u32[]{:S(2)}) collective-permute-start(f32[4,8,8,128]{3,2,1,0:T(8,128)S(1)} %reduce_sum.9.refs_0_), channel_id=1, source_target_pairs={{0,8},{8,0},{16,24},{24,16},{32,40},{40,32},{48,56},{56,48},{64,72... | collective-permute-start | bytes 393224 | tf_op jit(solution)/shard_map/ppermute | solution.py:223
  50.6 5.3 %collective-permute-start.17 = (f32[4,8,8,128]{3,2,1,0:T(8,128)S(1)}, f32[4,8,8,128]{3,2,1,0:T(8,128)S(1)}, u32[]{:S(2)}, u32[]{:S(2)}) collective-permute-start(f32[4,8,8,128]{3,2,1,0:T(8,128)S(1)} %collective-permute-done.16.refs_12_), channel_id=1, source_target_pairs={{0,8},{8,0},{16,24},{24,16},{32,40},{40,32},{48,56},{56,48},{64,72... | collective-permute-start | bytes 393224 | tf_op jit(solution)/shard_map/ppermute | solution.py:223
  51.5 5.8 %collective-permute-start.14 = (f32[4,8,8,128]{3,2,1,0:T(8,128)S(1)}, f32[4,8,8,128]{3,2,1,0:T(8,128)S(1)}, u32[]{:S(2)}, u32[]{:S(2)}) collective-permute-start(f32[4,8,8,128]{3,2,1,0:T(8,128)S(1)} %collective-permute-done.12.refs_8_), channel_id=1, source_target_pairs={{0,16},{8,24},{16,0},{24,8},{32,48},{40,56},{48,32},{56,40},{64,80... | collective-permute-start | bytes 393224 | tf_op jit(solution)/shard_map/ppermute | solution.py:223
  54.0 4.4 %collective-permute-start.13 = (f32[4,8,8,128]{3,2,1,0:T(8,128)S(1)}, f32[4,8,8,128]{3,2,1,0:T(8,128)S(1)}, u32[]{:S(2)}, u32[]{:S(2)}) collective-permute-start(f32[4,8,8,128]{3,2,1,0:T(8,128)S(1)} %collective-permute-done.12.refs_8_), channel_id=1, source_target_pairs={{0,8},{8,0},{16,24},{24,16},{32,40},{40,32},{48,56},{56,48},{64,72... | collective-permute-start | bytes 393224 | tf_op jit(solution)/shard_map/ppermute | solution.py:223
  54.3 6.0 %collective-permute-start.18 = (f32[4,8,8,128]{3,2,1,0:T(8,128)S(1)}, f32[4,8,8,128]{3,2,1,0:T(8,128)S(1)}, u32[]{:S(2)}, u32[]{:S(2)}) collective-permute-start(f32[4,8,8,128]{3,2,1,0:T(8,128)S(1)} %collective-permute-done.6.refs_2_), channel_id=1, source_target_pairs={{0,96},{8,104},{16,112},{24,120},{32,64},{40,72},{48,80},{56,88},{... | collective-permute-start | bytes 393224 | tf_op jit(solution)/shard_map/ppermute | solution.py:223
  55.9 5.5 %collective-permute-start.10 = (f32[4,8,8,128]{3,2,1,0:T(8,128)S(1)}, f32[4,8,8,128]{3,2,1,0:T(8,128)S(1)}, u32[]{:S(2)}, u32[]{:S(2)}) collective-permute-start(f32[4,8,8,128]{3,2,1,0:T(8,128)S(1)} %collective-permute-done.6.refs_2_), channel_id=1, source_target_pairs={{0,32},{8,40},{16,48},{24,56},{32,0},{40,8},{48,16},{56,24},{64,96... | collective-permute-start | bytes 393224 | tf_op jit(solution)/shard_map/ppermute | solution.py:223
  55.9 5.9 %collective-permute-start.7 = (f32[4,8,8,128]{3,2,1,0:T(8,128)S(1)}, f32[4,8,8,128]{3,2,1,0:T(8,128)S(1)}, u32[]{:S(2)}, u32[]{:S(2)}) collective-permute-start(f32[4,8,8,128]{3,2,1,0:T(8,128)S(1)} %collective-permute-done.6.refs_2_), channel_id=1, source_target_pairs={{0,8},{8,0},{16,24},{24,16},{32,40},{40,32},{48,56},{56,48},{64,72... | collective-permute-start | bytes 393224 | tf_op jit(solution)/shard_map/ppermute | solution.py:223
  57.3 4.6 %collective-permute-start.9 = (f32[4,8,8,128]{3,2,1,0:T(8,128)S(1)}, f32[4,8,8,128]{3,2,1,0:T(8,128)S(1)}, u32[]{:S(2)}, u32[]{:S(2)}) collective-permute-start(f32[4,8,8,128]{3,2,1,0:T(8,128)S(1)} %collective-permute-done.8.refs_4_), channel_id=1, source_target_pairs={{0,8},{8,0},{16,24},{24,16},{32,40},{40,32},{48,56},{56,48},{64,72... | collective-permute-start | bytes 393224 | tf_op jit(solution)/shard_map/ppermute | solution.py:223
  58.5 3.4 %collective-permute-start.15 = (f32[4,8,8,128]{3,2,1,0:T(8,128)S(1)}, f32[4,8,8,128]{3,2,1,0:T(8,128)S(1)}, u32[]{:S(2)}, u32[]{:S(2)}) collective-permute-start(f32[4,8,8,128]{3,2,1,0:T(8,128)S(1)} %collective-permute-done.14.refs_10_), channel_id=1, source_target_pairs={{0,8},{8,0},{16,24},{24,16},{32,40},{40,32},{48,56},{56,48},{64,72... | collective-permute-start | bytes 393224 | tf_op jit(solution)/shard_map/ppermute | solution.py:223
  60.3 2.1 %collective-permute-start.19 = (f32[4,8,8,128]{3,2,1,0:T(8,128)S(1)}, f32[4,8,8,128]{3,2,1,0:T(8,128)S(1)}, u32[]{:S(2)}, u32[]{:S(2)}) collective-permute-start(f32[4,8,8,128]{3,2,1,0:T(8,128)S(1)} %collective-permute-done.18.refs_14_), channel_id=1, source_target_pairs={{0,8},{8,0},{16,24},{24,16},{32,40},{40,32},{48,56},{56,48},{64,72... | collective-permute-start | bytes 393224 | tf_op jit(solution)/shard_map/ppermute | solution.py:223
  61.4 1.4 %collective-permute-start.11 = (f32[4,8,8,128]{3,2,1,0:T(8,128)S(1)}, f32[4,8,8,128]{3,2,1,0:T(8,128)S(1)}, u32[]{:S(2)}, u32[]{:S(2)}) collective-permute-start(f32[4,8,8,128]{3,2,1,0:T(8,128)S(1)} %collective-permute-done.10.refs_6_), channel_id=1, source_target_pairs={{0,8},{8,0},{16,24},{24,16},{32,40},{40,32},{48,56},{56,48},{64,72... | collective-permute-start | bytes 393224 | tf_op jit(solution)/shard_map/ppermute | solution.py:223

commit v2 on v0

--- a/solution.py
+++ b/solution.py
@@ -8,6 +8,8 @@
 
 
 TOPS = (5, 2, 2, 3, 3, 7)
+FIRST = (5, 3, 7, 4)
+SECOND = (1, 2, 6, 0)
 
 
 def coarse_position(numerator, level_now):
@@ -80,8 +82,9 @@
 
 
 def interp_kernel(levels, coefs, x, pf, *rest):
-    keep, send = rest[-2:]
-    core = lax.rem(lax.axis_index("grid"), 2)
+    keep, send, done = rest[-3:]
+    index = lax.axis_index("grid")
+    here, core = jnp.right_shift(index, 1), index & 1
     weight = coefs[0].astype(jnp.float32)
     short = [TOPS[k] - levels[0, k] for k in range(6)]
     matrix = pf[short[5]]
@@ -95,7 +98,7 @@
     sources, weights = two_sources(interp_tables(3))
     src1, src2 = (by_shortfall(sources[i], short[4]) for i in range(2))
     wt1, wt2 = (by_shortfall(weights[i], short[4]) * weight for i in range(2))
-    done = []
+    by_bc = []
     for bc in range(16):
         along_e = []
         for d in range(8):
@@ -103,17 +106,19 @@
             along_e.append(
                 wt1 * jnp.take_along_axis(tile, src1, axis=0) + wt2 * jnp.take_along_axis(tile, src2, axis=0)
             )
-        done.append(lead_interp(along_e, 3, short[3]))
+        by_bc.append(lead_interp(along_e, 3, short[3]))
     for d in range(8):
-        grid_now = [[done[b * 4 + c][d] for c in range(4)] for b in range(4)]
-        grid_now = [lead_interp(line, 2, short[2]) for line in grid_now]
-        columns = [lead_interp([grid_now[b][c] for b in range(4)], 2, short[1]) for c in range(4)]
-        for b in range(4):
-            for half in range(2):
-                even, odd = columns[2 * half][b], columns[2 * half + 1][b]
-                at = b * 2 + half
-                keep[at, 0, d] = jnp.where(core == 0, even, odd)
-                send[at, 0, d] = jnp.where(core == 0, odd, even)
+        lines = [lead_interp([by_bc[b * 4 + c][d] for c in range(4)], 2, short[2]) for b in range(4)]
+        for c in range(4):
+            for b, value in enumerate(lead_interp([lines[b][c] for b in range(4)], 2, short[1])):
+                done[b * 4 + c, d] = value
+    for i in range(4):
+        kept = jnp.where(core == 1, FIRST[i], SECOND[i]) ^ here
+        sent = jnp.where(core == 1, SECOND[i], FIRST[i]) ^ here
+        for c in range(2):
+            for d in range(8):
+                keep[i, 0, c, d] = done[kept * 2 + c, d]
+                send[i, 0, c, d] = done[sent * 2 + c, d]
 
 
 def in_vmem(x):
@@ -126,8 +131,8 @@
 
 def interp_rows(values, levels, coefs, matrices, first, count, after=()):
     smem = pl.BlockSpec(memory_space=pltpu.SMEM)
-    half = jax.ShapeDtypeStruct((8, count, 8, 8, 128), jnp.float32)
-    out_spec = pl.BlockSpec((8, 1, 8, 8, 128), lambda a: (0, a, 0, 0, 0))
+    half = jax.ShapeDtypeStruct((4, count, 2, 8, 8, 128), jnp.float32)
+    out_spec = pl.BlockSpec((4, 1, 2, 8, 8, 128), lambda a: (0, a, 0, 0, 0, 0))
     return pl.pallas_call(
         interp_kernel,
         grid=(count,),
@@ -140,30 +145,32 @@
         ],
         out_specs=[out_spec, out_spec],
         out_shape=[half, half],
+        scratch_shapes=[pltpu.VMEM((16, 8, 8, 128), jnp.float32)],
         compiler_params=pltpu.CompilerParams(vmem_limit_bytes=16 << 20),
         cost_estimate=pl.CostEstimate(flops=count * 10**8, bytes_accessed=count << 20, transcendentals=0),
     )(in_hbm(levels), coefs, in_hbm(values), in_hbm(matrices), *after)
 
 
-def combine_kernel(levels, others, own0, own123, got0, got123, next_own, next_got, out):
+def combine_kernel(levels, others, own0, own123, got0, got123, next_own, next_got, *outs):
     short = TOPS[0] - levels[0, 0]
     other_short = TOPS[0] - others[0, 0]
-    for at in range(8):
-        for d in range(8):
-            total = None
-            for zero, rest, after, miss in (
-                (own0, own123, next_own, short),
-                (got0, got123, next_got, other_short),
-            ):
-                start, end = zero[at, 0, d], after[at, 0, d]
-                one, two, three = (rest[at, i, d] for i in range(3))
-                two = jnp.where(miss >= 2, 0.5 * (start + end), two)
-                one = jnp.where(miss >= 1, 0.5 * (start + two), one)
-                three = jnp.where(miss >= 1, 0.5 * (two + end), three)
-                part = (start, one, two, three)
-                total = part if total is None else tuple(s + t for s, t in zip(total, part))
-            for i in range(4):
-                out[at, i, d] = total[i]
+    for at, out in enumerate(outs):
+        for c in range(2):
+            for d in range(8):
+                total = None
+                for zero, rest, after, miss in (
+                    (own0, own123, next_own, short),
+                    (got0, got123, next_got, other_short),
+                ):
+                    start, end = zero[at, 0, c, d], after[at, 0, c, d]
+                    one, two, three = (rest[at, i, c, d] for i in range(3))
+                    two = jnp.where(miss >= 2, 0.5 * (start + end), two)
+                    one = jnp.where(miss >= 1, 0.5 * (start + two), one)
+                    three = jnp.where(miss >= 1, 0.5 * (two + end), three)
+                    part = (start, one, two, three)
+                    total = part if total is None else tuple(s + t for s, t in zip(total, part))
+                for i in range(4):
+                    out[i, c, d] = total[i]
 
 
 def combine(levels, others, *pieces):
@@ -172,16 +179,16 @@
     return pl.pallas_call(
         combine_kernel,
         in_specs=[smem, smem, *[vmem] * len(pieces)],
-        out_specs=vmem,
-        out_shape=pltpu.VMEM((8, 4, 8, 8, 128), jnp.float32),
+        out_specs=[vmem] * 4,
+        out_shape=[pltpu.VMEM((4, 2, 8, 8, 128), jnp.float32)] * 4,
         compiler_params=pltpu.CompilerParams(vmem_limit_bytes=4 << 20),
         name="combine",
     )(levels, others, *[in_vmem(p) for p in pieces])
 
 
 def restrict_kernel(levels, *refs):
-    pieces, out, scratch, sems = refs[:16], *refs[16:]
-    index = lax.axis_index("grid")
+    north, south, out, scratch, sems = refs[:8], refs[8:16], *refs[16:]
+    here = jnp.right_shift(lax.axis_index("grid"), 1)
     short = [TOPS[k] - levels[0, k] for k in range(6)]
     spacing = jnp.left_shift(jnp.int32(1), short[0])
     sublane = lax.broadcasted_iota(jnp.int32, (8, 128), 0)
@@ -192,14 +199,16 @@
     copies = []
     for row in range(4):
         held_a = jnp.where(lax.rem(jnp.int32(row), spacing) == 0, 1.0, 0.0)
-        for slot, piece in enumerate(pieces):
-            at = index ^ slot
-            b, c = jnp.right_shift(at, 2), at & 3
-            held = jnp.where(
-                (b < jnp.right_shift(4, short[1])) & (c < jnp.right_shift(4, short[2])), held_a, 0.0
-            )
-            for d in range(8):
-                scratch[row, at, d] = piece[row, d] * (by_d[d] * held)
+        for slot in range(8):
+            for half in range(2):
+                at = (here ^ slot) * 2 + half
+                b, c = jnp.right_shift(at, 2), at & 3
+                held = jnp.where(
+                    (b < jnp.right_shift(4, short[1])) & (c < jnp.right_shift(4, short[2])), held_a, 0.0
+                )
+                for d in range(8):
+                    value = north[slot][row, half, d] + south[slot][row, half, d]
+                    scratch[row, at, d] = value * (by_d[d] * held)
         copies.append(pltpu.make_async_copy(scratch.at[row], out.at[row], sems.at[row]))
         copies[-1].start()
     for copy in copies:
@@ -223,6 +232,14 @@
     return lax.ppermute(x, "grid", [(i, i ^ bits) for i in range(16)])
 
 
+def between(x, bits, cores):
+    return lax.ppermute(x, "grid", [(h * 2 + core, (h ^ bits) * 2 + core) for h in range(8) for core in cores])
+
+
+def across(x, core):
+    return lax.ppermute(x, "grid", [(h * 2 + core, h * 2 + 1 - core) for h in range(8)])
+
+
 def to_previous(x, bits):
     pairs = [(r * 8 + d, (r ^ bits) * 8 + (d - 1) % 8) for r in range(16) for d in range(8)]
     return lax.ppermute(x, ("grid", "dom"), pairs)
@@ -237,15 +254,27 @@
     keep123, send123 = interp_rows(values, levels, coefficients, matrices, 1, 3, (keep0,))
     got0, got123 = swap(send0, 1), swap(send123, 1)
     parts = combine(levels, others, keep0, keep123, got0, got123, next_own, next_got)
-    groups = [[h * 2 + core for h in range(8)] for core in range(2)]
-    arrived = lax.all_to_all(parts, "grid", split_axis=0, concat_axis=0, axis_index_groups=groups, tiled=True)
-    share = arrived.sum(axis=0)
-    pieces = {0: share}
-    for bits in (4, 12, 2, 6, 14, 8, 10):
-        pieces[bits] = swap(share, bits)
-    for bits in list(pieces):
-        pieces[bits + 1] = swap(pieces[bits], 1)
-    return restrict(levels, [pieces[slot] for slot in range(16)])
+    for_y2 = lax.optimization_barrier(parts[3]) + between(parts[0], 1, (1,))
+    arrived = between(parts[1], 2, (0, 1))
+    arrived = arrived + between(parts[2], 6, (0, 1))
+    own_z = across(parts[0], 0)
+    share = between(for_y2, 4, (1,))
+    share = share + between(own_z + arrived, 1, (1,))
+    share = share + across(parts[3] + arrived, 0)
+    north, south = {0: share}, {}
+    north[1] = between(share, 1, (1,))
+    south[0] = across(share, 1)
+    north[4] = between(share, 4, (1,))
+    south[2] = between(south[0], 2, (0,))
+    south[6] = between(south[0], 6, (0,))
+    north[3] = between(north[1], 2, (1,))
+    north[7] = between(north[1], 6, (1,))
+    north[5] = between(north[4], 1, (1,))
+    for slot in (1, 4, 3, 7, 5):
+        south[slot] = across(north[slot], 1)
+    for slot in (2, 6):
+        north[slot] = across(south[slot], 0)
+    return restrict(levels, [north[slot] for slot in range(8)] + [south[slot] for slot in range(8)])
 
 
 def solution(mesh):

time: 67.7 us -> 79.7 us (1.18)
  starting transfers between devices: 28.8 us -> 50.5 us
  blocking collectives: 18.3 us -> 0 us
  waiting for transfers between devices: 12.3 us -> 20 us
    ppermute x0 -> x22, starting transfers between devices: none -> 42.3 us  [the longest x12 27.6 us: between(): lax.ppermute(x, 'grid', [(h * 2 + core, (h ^ bits) * 2 + core) for h in r...]
    ppermute x18 -> x3, starting transfers between devices: 22.9 us -> 2.29 us  [swap(): return lax.ppermute(x, 'grid', [(i, i ^ bits) for i in range(16)])]
    all_to_all x1 -> x0, blocking collectives: 18.3 us -> none  [whole(): lax.all_to_all(parts, 'grid', split_axis=0, concat_axis=0, axis_index_gro...]
    ppermute x0 -> x22, waiting for transfers between devices: none -> 9.69 us  [the longest x12 8.58 us: between(): lax.ppermute(x, 'grid', [(h * 2 + core, (h ^ bits) * 2 + core) for h in r...]
    ppermute x18 -> x3, waiting for transfers between devices: 2.81 us -> 0.82 us  [swap(): return lax.ppermute(x, 'grid', [(i, i ^ bits) for i in range(16)])]
  transfers between devices with their start and end apart: 20 -> 27, of which waited for: 8 -> 7; matrix products, arithmetic and copies ran while one was open for 0% -> 0% of each run, Pallas kernels for 0% -> 0%
where the time goes in v2:
time: 79.7 us; the launch traced here: 79.2 us
  starting transfers between devices  50.5 us (63%)
  waiting for transfers between devices  20 us (25%)
  Pallas kernels  7.56 us (9%)
  between operations  0.99 us (1%)
    ppermute x12, starting transfers between devices, between(): lax.ppermute(x, 'grid', [(h * 2 + core, (h ^ bits) * 2 + core) for h in r...  27.6 us
    ppermute x10, starting transfers between devices, across(): lax.ppermute(x, 'grid', [(h * 2 + core, h * 2 + 1 - core) for h in range(...  14.7 us
    ppermute x2, waiting for transfers between devices, to_previous(): return lax.ppermute(x, ('grid', 'dom'), pairs)  9.48 us
    ppermute x12, waiting for transfers between devices, between(): lax.ppermute(x, 'grid', [(h * 2 + core, (h ^ bits) * 2 + core) for h in r...  8.58 us
    ppermute x2, starting transfers between devices, to_previous(): return lax.ppermute(x, ('grid', 'dom'), pairs)  5.87 us
    pallas_call x2, Pallas kernels, interp_rows(): pl.pallas_call(interp_kernel, grid=(count,), in_specs=[smem, smem, pl.Blo...  4.51 us
    ppermute x3, starting transfers between devices, swap(): return lax.ppermute(x, 'grid', [(i, i ^ bits) for i in range(16)])  2.29 us
    pallas_call x1, Pallas kernels, restrict(): pl.pallas_call(restrict_kernel, in_specs=[pl.BlockSpec(memory_space=pltpu...  2.27 us
  transfers between devices with their start and end apart: 27, of which 7 were waited for; matrix products, arithmetic and copies ran while one was open for 0% of the time, Pallas kernels for 0%

profile of v2, /device:TPU:1, one launch (start us, length us, event | category | flops | bytes accessed | tf_op | source)
XLA Modules:
  0.0 79.2 jit_solution(18374016569202595978)
XLA Ops:
  0.7 1.5 %shard_map.46 = (f32[4,1,2,8,8,128]{5,4,3,2,1,0:T(8,128)S(1)}, f32[4,1,2,8,8,128]{5,4,3,2,1,0:T(8,128)S(1)}) custom-call(s32[1,6]{1,0:T(1,128)} %levels.7, s32[1]{0:T(128)S(6)} %copy.5.coefs, f32[1,4,4,4,8,8,128]{6,5,4,3,2,1,0:T(8,128)} %x.3, bf16[3,128,128]{2,1,0:T(8,128)(2,1)} %constant.2.clone.pf), custom_call_target="tpu_custom_call" | custom-call | flops 100000000 | bytes 1048576 | tf_op jit(solution)/shard_map/pallas_call | solution.py:136
  2.1 3.1 %shard_map.47 = (f32[4,3,2,8,8,128]{5,4,3,2,1,0:T(8,128)S(1)}, f32[4,3,2,8,8,128]{5,4,3,2,1,0:T(8,128)S(1)}) custom-call(s32[1,6]{1,0:T(1,128)} %levels.7, s32[1]{0:T(128)S(6)} %copy.5.coefs, f32[1,4,4,4,8,8,128]{6,5,4,3,2,1,0:T(8,128)} %x.3, bf16[3,128,128]{2,1,0:T(8,128)(2,1)} %constant.2.clone.pf, f32[4,1,2,8,8,128]{5,4,3,2,1,0:T(8,128)S(1)} %get-tuple-element.13.rest_0_.own0), custom_call_target="tpu_custom_call" | custom-call | flops 300000000 | bytes 3145728 | tf_op jit(solution)/shard_map/pallas_call | solution.py:136
  5.2 1.5 %collective-permute-start.2 = (f32[4,3,2,8,8,128]{5,4,3,2,1,0:T(8,128)S(1)}, f32[4,3,2,8,8,128]{5,4,3,2,1,0:T(8,128)S(1)}, u32[]{:S(2)}, u32[]{:S(2)}) collective-permute-start(f32[4,3,2,8,8,128]{5,4,3,2,1,0:T(8,128)S(1)} %get-tuple-element.16), channel_id=1, source_target_pairs={{0,8},{8,0},{16,24},{24,16},{32,40},{40,32},{48,56},{56,48},{64,72... | collective-permute-start | bytes 2359304 | tf_op jit(solution)/shard_map/ppermute | solution.py:232
  6.7 5.9 %collective-permute-start.4 = (f32[4,1,2,8,8,128]{5,4,3,2,1,0:T(8,128)S(1)}, f32[4,1,2,8,8,128]{5,4,3,2,1,0:T(8,128)S(1)}, u32[]{:S(2)}, u32[]{:S(2)}) collective-permute-start(f32[4,1,2,8,8,128]{5,4,3,2,1,0:T(8,128)S(1)} %get-tuple-element.15), channel_id=1, source_target_pairs={{0,15},{1,8},{2,9},{3,10},{4,11},{5,12},{6,13},{7,14},{8,7},{9,0},... | collective-permute-start | bytes 786440 | tf_op jit(solution)/shard_map/ppermute | solution.py:245
  13.4 0.8 %collective-permute-done.others = s32[1,6]{1,0:T(1,128)S(1)} collective-permute-done((s32[1,6]{1,0:T(1,128)S(1)}, s32[1,6]{1,0:T(1,128)S(1)}, u32[]{:S(2)}, u32[]{:S(2)}) %collective-permute-start) | collective-permute-done | bytes 56 | tf_op jit(solution)/shard_map/ppermute | solution.py:232
  14.2 3.9 %collective-permute-done.4.next_got = f32[4,1,2,8,8,128]{5,4,3,2,1,0:T(8,128)S(1)} collective-permute-done((f32[4,1,2,8,8,128]{5,4,3,2,1,0:T(8,128)S(1)}, f32[4,1,2,8,8,128]{5,4,3,2,1,0:T(8,128)S(1)}, u32[]{:S(2)}, u32[]{:S(2)}) %collective-permute-start.4) | collective-permute-done | bytes 262176 | tf_op jit(solution)/shard_map/ppermute | solution.py:245
  18.0 5.6 %collective-permute-done.3.next_own = f32[4,1,2,8,8,128]{5,4,3,2,1,0:T(8,128)S(1)} collective-permute-done((f32[4,1,2,8,8,128]{5,4,3,2,1,0:T(8,128)S(1)}, f32[4,1,2,8,8,128]{5,4,3,2,1,0:T(8,128)S(1)}, u32[]{:S(2)}, u32[]{:S(2)}) %collective-permute-start.3) | collective-permute-done | bytes 262176 | tf_op jit(solution)/shard_map/ppermute | solution.py:245
  24.4 1.4 %collective-permute-start.8 = (f32[4,2,8,8,128]{4,3,2,1,0:T(8,128)S(1)}, f32[4,2,8,8,128]{4,3,2,1,0:T(8,128)S(1)}, u32[]{:S(2)}, u32[]{:S(2)}) collective-permute-start(f32[4,2,8,8,128]{4,3,2,1,0:T(8,128)S(1)} %get-tuple-element.19), channel_id=1, source_target_pairs={{0,32},{8,40},{16,48},{24,56},{32,0},{40,8},{48,16},{56,24},{64,96... | collective-permute-start | bytes 786440 | tf_op jit(solution)/shard_map/ppermute | solution.py:236
  25.8 1.9 %collective-permute-start.9 = (f32[4,2,8,8,128]{4,3,2,1,0:T(8,128)S(1)}, f32[4,2,8,8,128]{4,3,2,1,0:T(8,128)S(1)}, u32[]{:S(2)}, u32[]{:S(2)}) collective-permute-start(f32[4,2,8,8,128]{4,3,2,1,0:T(8,128)S(1)} %get-tuple-element.20), channel_id=1, source_target_pairs={{0,96},{8,104},{16,112},{24,120},{32,64},{40,72},{48,80},{56,88},{... | collective-permute-start | bytes 786440 | tf_op jit(solution)/shard_map/ppermute | solution.py:236
  27.7 1.3 %collective-permute-start.7 = (f32[4,2,8,8,128]{4,3,2,1,0:T(8,128)S(1)}, f32[4,2,8,8,128]{4,3,2,1,0:T(8,128)S(1)}, u32[]{:S(2)}, u32[]{:S(2)}) collective-permute-start(f32[4,2,8,8,128]{4,3,2,1,0:T(8,128)S(1)} %get-tuple-element.18), channel_id=1, source_target_pairs={{0,8},{16,24},{32,40},{48,56},{64,72},{80,88},{96,104},{112,120},{... | collective-permute-start | bytes 786440 | tf_op jit(solution)/shard_map/ppermute | solution.py:240
  29.0 2.7 %collective-permute-start.5 = (f32[4,2,8,8,128]{4,3,2,1,0:T(8,128)S(1)}, f32[4,2,8,8,128]{4,3,2,1,0:T(8,128)S(1)}, u32[]{:S(2)}, u32[]{:S(2)}) collective-permute-start(f32[4,2,8,8,128]{4,3,2,1,0:T(8,128)S(1)} %get-tuple-element.18), channel_id=1, source_target_pairs={{8,24},{24,8},{40,56},{56,40},{72,88},{88,72},{104,120},{120,104},... | collective-permute-start | bytes 786440 | tf_op jit(solution)/shard_map/ppermute | solution.py:236
  31.7 1.9 %collective-permute-done.9 = f32[4,2,8,8,128]{4,3,2,1,0:T(8,128)S(1)} collective-permute-done((f32[4,2,8,8,128]{4,3,2,1,0:T(8,128)S(1)}, f32[4,2,8,8,128]{4,3,2,1,0:T(8,128)S(1)}, u32[]{:S(2)}, u32[]{:S(2)}) %collective-permute-start.9) | collective-permute-done | bytes 262176 | tf_op jit(solution)/shard_map/ppermute | solution.py:236
  33.7 2.7 %collective-permute-start.10 = (f32[4,2,8,8,128]{4,3,2,1,0:T(8,128)S(1)}, f32[4,2,8,8,128]{4,3,2,1,0:T(8,128)S(1)}, u32[]{:S(2)}, u32[]{:S(2)}) collective-permute-start(f32[4,2,8,8,128]{4,3,2,1,0:T(8,128)S(1)} %get-tuple-element.21), channel_id=1, source_target_pairs={{8,24},{24,8},{40,56},{56,40},{72,88},{88,72},{104,120},{120,104},... | collective-permute-start | bytes 786440 | tf_op jit(solution)/shard_map/ppermute | solution.py:236
  36.4 1.3 %collective-permute-start.11 = (f32[4,2,8,8,128]{4,3,2,1,0:T(8,128)S(1)}, f32[4,2,8,8,128]{4,3,2,1,0:T(8,128)S(1)}, u32[]{:S(2)}, u32[]{:S(2)}) collective-permute-start(f32[4,2,8,8,128]{4,3,2,1,0:T(8,128)S(1)} %get-tuple-element.22), channel_id=1, source_target_pairs={{0,8},{16,24},{32,40},{48,56},{64,72},{80,88},{96,104},{112,120},{... | collective-permute-start | bytes 786440 | tf_op jit(solution)/shard_map/ppermute | solution.py:240
  37.7 3.3 %collective-permute-start.6 = (f32[4,2,8,8,128]{4,3,2,1,0:T(8,128)S(1)}, f32[4,2,8,8,128]{4,3,2,1,0:T(8,128)S(1)}, u32[]{:S(2)}, u32[]{:S(2)}) collective-permute-start(f32[4,2,8,8,128]{4,3,2,1,0:T(8,128)S(1)} %add.18), channel_id=1, source_target_pairs={{8,72},{24,88},{40,104},{56,120},{72,8},{88,24},{104,40},{120,56},... | collective-permute-start | bytes 786440 | tf_op jit(solution)/shard_map/ppermute | solution.py:236
  41.1 5.3 %collective-permute-done.6 = f32[4,2,8,8,128]{4,3,2,1,0:T(8,128)S(1)} collective-permute-done((f32[4,2,8,8,128]{4,3,2,1,0:T(8,128)S(1)}, f32[4,2,8,8,128]{4,3,2,1,0:T(8,128)S(1)}, u32[]{:S(2)}, u32[]{:S(2)}) %collective-permute-start.6) | collective-permute-done | bytes 262176 | tf_op jit(solution)/shard_map/ppermute | solution.py:236
  46.4 3.3 %collective-permute-start.17 = (f32[4,2,8,8,128]{4,3,2,1,0:T(8,128)S(1)}, f32[4,2,8,8,128]{4,3,2,1,0:T(8,128)S(1)}, u32[]{:S(2)}, u32[]{:S(2)}) collective-permute-start(f32[4,2,8,8,128]{4,3,2,1,0:T(8,128)S(1)} %add_add_fusion.refs_0_), channel_id=1, source_target_pairs={{8,72},{24,88},{40,104},{56,120},{72,8},{88,24},{104,40},{120,56},... | collective-permute-start | bytes 786440 | tf_op jit(solution)/shard_map/ppermute | solution.py:236
  49.7 1.3 %collective-permute-start.13 = (f32[4,2,8,8,128]{4,3,2,1,0:T(8,128)S(1)}, f32[4,2,8,8,128]{4,3,2,1,0:T(8,128)S(1)}, u32[]{:S(2)}, u32[]{:S(2)}) collective-permute-start(f32[4,2,8,8,128]{4,3,2,1,0:T(8,128)S(1)} %add_add_fusion.refs_0_), channel_id=1, source_target_pairs={{8,0},{24,16},{40,32},{56,48},{72,64},{88,80},{104,96},{120,112},{... | collective-permute-start | bytes 786440 | tf_op jit(solution)/shard_map/ppermute | solution.py:240
  51.0 2.6 %collective-permute-start.12 = (f32[4,2,8,8,128]{4,3,2,1,0:T(8,128)S(1)}, f32[4,2,8,8,128]{4,3,2,1,0:T(8,128)S(1)}, u32[]{:S(2)}, u32[]{:S(2)}) collective-permute-start(f32[4,2,8,8,128]{4,3,2,1,0:T(8,128)S(1)} %add_add_fusion.refs_0_), channel_id=1, source_target_pairs={{8,24},{24,8},{40,56},{56,40},{72,88},{88,72},{104,120},{120,104},... | collective-permute-start | bytes 786440 | tf_op jit(solution)/shard_map/ppermute | solution.py:236
  53.6 1.4 %collective-permute-done.17.refs_4_ = f32[4,2,8,8,128]{4,3,2,1,0:T(8,128)S(1)} collective-permute-done((f32[4,2,8,8,128]{4,3,2,1,0:T(8,128)S(1)}, f32[4,2,8,8,128]{4,3,2,1,0:T(8,128)S(1)}, u32[]{:S(2)}, u32[]{:S(2)}) %collective-permute-start.17) | collective-permute-done | bytes 262176 | tf_op jit(solution)/shard_map/ppermute | solution.py:236
  55.0 1.3 %collective-permute-start.24 = (f32[4,2,8,8,128]{4,3,2,1,0:T(8,128)S(1)}, f32[4,2,8,8,128]{4,3,2,1,0:T(8,128)S(1)}, u32[]{:S(2)}, u32[]{:S(2)}) collective-permute-start(f32[4,2,8,8,128]{4,3,2,1,0:T(8,128)S(1)} %collective-permute-done.17.refs_4_), channel_id=1, source_target_pairs={{8,0},{24,16},{40,32},{56,48},{72,64},{88,80},{104,96},{120,112},{... | collective-permute-start | bytes 786440 | tf_op jit(solution)/shard_map/ppermute | solution.py:240
  56.3 2.6 %collective-permute-start.18 = (f32[4,2,8,8,128]{4,3,2,1,0:T(8,128)S(1)}, f32[4,2,8,8,128]{4,3,2,1,0:T(8,128)S(1)}, u32[]{:S(2)}, u32[]{:S(2)}) collective-permute-start(f32[4,2,8,8,128]{4,3,2,1,0:T(8,128)S(1)} %collective-permute-done.17.refs_4_), channel_id=1, source_target_pairs={{8,24},{24,8},{40,56},{56,40},{72,88},{88,72},{104,120},{120,104},... | collective-permute-start | bytes 786440 | tf_op jit(solution)/shard_map/ppermute | solution.py:236
  60.3 1.3 %collective-permute-start.22 = (f32[4,2,8,8,128]{4,3,2,1,0:T(8,128)S(1)}, f32[4,2,8,8,128]{4,3,2,1,0:T(8,128)S(1)}, u32[]{:S(2)}, u32[]{:S(2)}) collective-permute-start(f32[4,2,8,8,128]{4,3,2,1,0:T(8,128)S(1)} %collective-permute-done.12.refs_1_), channel_id=1, source_target_pairs={{8,0},{24,16},{40,32},{56,48},{72,64},{88,80},{104,96},{120,112},{... | collective-permute-start | bytes 786440 | tf_op jit(solution)/shard_map/ppermute | solution.py:240
  61.6 3.8 %collective-permute-start.21 = (f32[4,2,8,8,128]{4,3,2,1,0:T(8,128)S(1)}, f32[4,2,8,8,128]{4,3,2,1,0:T(8,128)S(1)}, u32[]{:S(2)}, u32[]{:S(2)}) collective-permute-start(f32[4,2,8,8,128]{4,3,2,1,0:T(8,128)S(1)} %collective-permute-done.12.refs_1_), channel_id=1, source_target_pairs={{8,104},{24,120},{40,72},{56,88},{72,40},{88,56},{104,8},{120,24},... | collective-permute-start | bytes 786440 | tf_op jit(solution)/shard_map/ppermute | solution.py:236
  65.5 1.9 %collective-permute-start.16 = (f32[4,2,8,8,128]{4,3,2,1,0:T(8,128)S(1)}, f32[4,2,8,8,128]{4,3,2,1,0:T(8,128)S(1)}, u32[]{:S(2)}, u32[]{:S(2)}) collective-permute-start(f32[4,2,8,8,128]{4,3,2,1,0:T(8,128)S(1)} %collective-permute-done.12.refs_1_), channel_id=1, source_target_pairs={{8,40},{24,56},{40,8},{56,24},{72,104},{88,120},{104,72},{120,88},... | collective-permute-start | bytes 786440 | tf_op jit(solution)/shard_map/ppermute | solution.py:236
  67.4 1.3 %collective-permute-start.25 = (f32[4,2,8,8,128]{4,3,2,1,0:T(8,128)S(1)}, f32[4,2,8,8,128]{4,3,2,1,0:T(8,128)S(1)}, u32[]{:S(2)}, u32[]{:S(2)}) collective-permute-start(f32[4,2,8,8,128]{4,3,2,1,0:T(8,128)S(1)} %collective-permute-done.18.refs_5_), channel_id=1, source_target_pairs={{8,0},{24,16},{40,32},{56,48},{72,64},{88,80},{104,96},{120,112},{... | collective-permute-start | bytes 786440 | tf_op jit(solution)/shard_map/ppermute | solution.py:240
  68.7 1.3 %collective-permute-start.20 = (f32[4,2,8,8,128]{4,3,2,1,0:T(8,128)S(1)}, f32[4,2,8,8,128]{4,3,2,1,0:T(8,128)S(1)}, u32[]{:S(2)}, u32[]{:S(2)}) collective-permute-start(f32[4,2,8,8,128]{4,3,2,1,0:T(8,128)S(1)} %collective-permute-done.19.refs_14_), channel_id=1, source_target_pairs={{0,8},{16,24},{32,40},{48,56},{64,72},{80,88},{96,104},{112,120},{... | collective-permute-start | bytes 786440 | tf_op jit(solution)/shard_map/ppermute | solution.py:240
  70.0 1.3 %collective-permute-start.15 = (f32[4,2,8,8,128]{4,3,2,1,0:T(8,128)S(1)}, f32[4,2,8,8,128]{4,3,2,1,0:T(8,128)S(1)}, u32[]{:S(2)}, u32[]{:S(2)}) collective-permute-start(f32[4,2,8,8,128]{4,3,2,1,0:T(8,128)S(1)} %collective-permute-done.14.refs_10_), channel_id=1, source_target_pairs={{0,8},{16,24},{32,40},{48,56},{64,72},{80,88},{96,104},{112,120},{... | collective-permute-start | bytes 786440 | tf_op jit(solution)/shard_map/ppermute | solution.py:240
  71.4 3.1 %collective-permute-start.26 = (f32[4,2,8,8,128]{4,3,2,1,0:T(8,128)S(1)}, f32[4,2,8,8,128]{4,3,2,1,0:T(8,128)S(1)}, u32[]{:S(2)}, u32[]{:S(2)}) collective-permute-start(f32[4,2,8,8,128]{4,3,2,1,0:T(8,128)S(1)} %collective-permute-done.21.refs_7_), channel_id=1, source_target_pairs={{8,0},{24,16},{40,32},{56,48},{72,64},{88,80},{104,96},{120,112},{... | collective-permute-start | bytes 786440 | tf_op jit(solution)/shard_map/ppermute | solution.py:240
  74.4 1.3 %collective-permute-start.23 = (f32[4,2,8,8,128]{4,3,2,1,0:T(8,128)S(1)}, f32[4,2,8,8,128]{4,3,2,1,0:T(8,128)S(1)}, u32[]{:S(2)}, u32[]{:S(2)}) collective-permute-start(f32[4,2,8,8,128]{4,3,2,1,0:T(8,128)S(1)} %collective-permute-done.16.refs_3_), channel_id=1, source_target_pairs={{8,0},{24,16},{40,32},{56,48},{72,64},{88,80},{104,96},{120,112},{... | collective-permute-start | bytes 786440 | tf_op jit(solution)/shard_map/ppermute | solution.py:240
  75.8 1.1 %collective-permute-done.23.refs_11_ = f32[4,2,8,8,128]{4,3,2,1,0:T(8,128)S(1)} collective-permute-done((f32[4,2,8,8,128]{4,3,2,1,0:T(8,128)S(1)}, f32[4,2,8,8,128]{4,3,2,1,0:T(8,128)S(1)}, u32[]{:S(2)}, u32[]{:S(2)}) %collective-permute-start.23) | collective-permute-done | bytes 262176 | tf_op jit(solution)/shard_map/ppermute | solution.py:240
  76.9 2.3 %restrict.1 = f32[4,16,8,8,128]{4,3,2,1,0:T(8,128)} custom-call(s32[1,6]{1,0:T(1,128)S(1)} %copy-done, f32[4,2,8,8,128]{4,3,2,1,0:T(8,128)S(1)} %add_add_fusion.refs_0_, f32[4,2,8,8,128]{4,3,2,1,0:T(8,128)S(1)} %collective-permute-done.12.refs_1_, f32[4,2,8,8,128]{4,3,2,1,0:T(8,128)S(1)} %collective-permute-done.15.refs_2_, ...), custom_call_target="tpu_custom_call" | custom-call | tf_op jit(solution)/shard_map/restrict/pallas_call | solution.py:219
  (31 shorter events, 3.2 us)
Async XLA Ops:
  0.7 12.3 %copy-start = (s32[1,6]{1,0:T(1,128)S(1)}, s32[1,6]{1,0:T(1,128)}, u32[]{:S(2)}) copy-start(s32[1,6]{1,0:T(1,128)} %levels.7) | copy-start | bytes 76
  5.2 18.5 %collective-permute-start.2 = (f32[4,3,2,8,8,128]{5,4,3,2,1,0:T(8,128)S(1)}, f32[4,3,2,8,8,128]{5,4,3,2,1,0:T(8,128)S(1)}, u32[]{:S(2)}, u32[]{:S(2)}) collective-permute-start(f32[4,3,2,8,8,128]{5,4,3,2,1,0:T(8,128)S(1)} %get-tuple-element.16), channel_id=1, source_target_pairs={{0,8},{8,0},{16,24},{24,16},{32,40},{40,32},{48,56},{56,48},{64,72... | collective-permute-start | bytes 2359304 | tf_op jit(solution)/shard_map/ppermute | solution.py:232
  6.7 11.4 %collective-permute-start.4 = (f32[4,1,2,8,8,128]{5,4,3,2,1,0:T(8,128)S(1)}, f32[4,1,2,8,8,128]{5,4,3,2,1,0:T(8,128)S(1)}, u32[]{:S(2)}, u32[]{:S(2)}) collective-permute-start(f32[4,1,2,8,8,128]{5,4,3,2,1,0:T(8,128)S(1)} %get-tuple-element.15), channel_id=1, source_target_pairs={{0,15},{1,8},{2,9},{3,10},{4,11},{5,12},{6,13},{7,14},{8,7},{9,0},... | collective-permute-start | bytes 786440 | tf_op jit(solution)/shard_map/ppermute | solution.py:245
  12.5 5.5 %collective-permute-start.1 = (f32[4,1,2,8,8,128]{5,4,3,2,1,0:T(8,128)S(1)}, f32[4,1,2,8,8,128]{5,4,3,2,1,0:T(8,128)S(1)}, u32[]{:S(2)}, u32[]{:S(2)}) collective-permute-start(f32[4,1,2,8,8,128]{5,4,3,2,1,0:T(8,128)S(1)} %get-tuple-element.15), channel_id=1, source_target_pairs={{0,8},{8,0},{16,24},{24,16},{32,40},{40,32},{48,56},{56,48},{64,72... | collective-permute-start | bytes 786440 | tf_op jit(solution)/shard_map/ppermute | solution.py:232
  13.0 10.7 %collective-permute-start.3 = (f32[4,1,2,8,8,128]{5,4,3,2,1,0:T(8,128)S(1)}, f32[4,1,2,8,8,128]{5,4,3,2,1,0:T(8,128)S(1)}, u32[]{:S(2)}, u32[]{:S(2)}) collective-permute-start(f32[4,1,2,8,8,128]{5,4,3,2,1,0:T(8,128)S(1)} %get-tuple-element.13.rest_0_.own0), channel_id=1, source_target_pairs={{0,7},{1,0},{2,1},{3,2},{4,3},{5,4},{6,5},{7,6},{8,15},{9,8},{10,9... | collective-permute-start | bytes 786440 | tf_op jit(solution)/shard_map/ppermute | solution.py:245
  13.0 1.2 %collective-permute-start = (s32[1,6]{1,0:T(1,128)S(1)}, s32[1,6]{1,0:T(1,128)S(1)}, u32[]{:S(2)}, u32[]{:S(2)}) collective-permute-start(s32[1,6]{1,0:T(1,128)S(1)} %copy-done), channel_id=1, source_target_pairs={{0,8},{8,0},{16,24},{24,16},{32,40},{40,32},{48,56},{56,48},{64,72... | collective-permute-start | bytes 80 | tf_op jit(solution)/shard_map/ppermute | solution.py:232
  24.4 7.2 %collective-permute-start.8 = (f32[4,2,8,8,128]{4,3,2,1,0:T(8,128)S(1)}, f32[4,2,8,8,128]{4,3,2,1,0:T(8,128)S(1)}, u32[]{:S(2)}, u32[]{:S(2)}) collective-permute-start(f32[4,2,8,8,128]{4,3,2,1,0:T(8,128)S(1)} %get-tuple-element.19), channel_id=1, source_target_pairs={{0,32},{8,40},{16,48},{24,56},{32,0},{40,8},{48,16},{56,24},{64,96... | collective-permute-start | bytes 786440 | tf_op jit(solution)/shard_map/ppermute | solution.py:236
  25.8 7.8 %collective-permute-start.9 = (f32[4,2,8,8,128]{4,3,2,1,0:T(8,128)S(1)}, f32[4,2,8,8,128]{4,3,2,1,0:T(8,128)S(1)}, u32[]{:S(2)}, u32[]{:S(2)}) collective-permute-start(f32[4,2,8,8,128]{4,3,2,1,0:T(8,128)S(1)} %get-tuple-element.20), channel_id=1, source_target_pairs={{0,96},{8,104},{16,112},{24,120},{32,64},{40,72},{48,80},{56,88},{... | collective-permute-start | bytes 786440 | tf_op jit(solution)/shard_map/ppermute | solution.py:236
  27.7 5.9 %collective-permute-start.7 = (f32[4,2,8,8,128]{4,3,2,1,0:T(8,128)S(1)}, f32[4,2,8,8,128]{4,3,2,1,0:T(8,128)S(1)}, u32[]{:S(2)}, u32[]{:S(2)}) collective-permute-start(f32[4,2,8,8,128]{4,3,2,1,0:T(8,128)S(1)} %get-tuple-element.18), channel_id=1, source_target_pairs={{0,8},{16,24},{32,40},{48,56},{64,72},{80,88},{96,104},{112,120},{... | collective-permute-start | bytes 786440 | tf_op jit(solution)/shard_map/ppermute | solution.py:240
  29.0 8.7 %collective-permute-start.5 = (f32[4,2,8,8,128]{4,3,2,1,0:T(8,128)S(1)}, f32[4,2,8,8,128]{4,3,2,1,0:T(8,128)S(1)}, u32[]{:S(2)}, u32[]{:S(2)}) collective-permute-start(f32[4,2,8,8,128]{4,3,2,1,0:T(8,128)S(1)} %get-tuple-element.18), channel_id=1, source_target_pairs={{8,24},{24,8},{40,56},{56,40},{72,88},{88,72},{104,120},{120,104},... | collective-permute-start | bytes 786440 | tf_op jit(solution)/shard_map/ppermute | solution.py:236
  33.7 7.3 %collective-permute-start.10 = (f32[4,2,8,8,128]{4,3,2,1,0:T(8,128)S(1)}, f32[4,2,8,8,128]{4,3,2,1,0:T(8,128)S(1)}, u32[]{:S(2)}, u32[]{:S(2)}) collective-permute-start(f32[4,2,8,8,128]{4,3,2,1,0:T(8,128)S(1)} %get-tuple-element.21), channel_id=1, source_target_pairs={{8,24},{24,8},{40,56},{56,40},{72,88},{88,72},{104,120},{120,104},... | collective-permute-start | bytes 786440 | tf_op jit(solution)/shard_map/ppermute | solution.py:236
  36.4 4.7 %collective-permute-start.11 = (f32[4,2,8,8,128]{4,3,2,1,0:T(8,128)S(1)}, f32[4,2,8,8,128]{4,3,2,1,0:T(8,128)S(1)}, u32[]{:S(2)}, u32[]{:S(2)}) collective-permute-start(f32[4,2,8,8,128]{4,3,2,1,0:T(8,128)S(1)} %get-tuple-element.22), channel_id=1, source_target_pairs={{0,8},{16,24},{32,40},{48,56},{64,72},{80,88},{96,104},{112,120},{... | collective-permute-start | bytes 786440 | tf_op jit(solution)/shard_map/ppermute | solution.py:240
  37.7 8.6 %collective-permute-start.6 = (f32[4,2,8,8,128]{4,3,2,1,0:T(8,128)S(1)}, f32[4,2,8,8,128]{4,3,2,1,0:T(8,128)S(1)}, u32[]{:S(2)}, u32[]{:S(2)}) collective-permute-start(f32[4,2,8,8,128]{4,3,2,1,0:T(8,128)S(1)} %add.18), channel_id=1, source_target_pairs={{8,72},{24,88},{40,104},{56,120},{72,8},{88,24},{104,40},{120,56},... | collective-permute-start | bytes 786440 | tf_op jit(solution)/shard_map/ppermute | solution.py:236
  46.4 8.6 %collective-permute-start.17 = (f32[4,2,8,8,128]{4,3,2,1,0:T(8,128)S(1)}, f32[4,2,8,8,128]{4,3,2,1,0:T(8,128)S(1)}, u32[]{:S(2)}, u32[]{:S(2)}) collective-permute-start(f32[4,2,8,8,128]{4,3,2,1,0:T(8,128)S(1)} %add_add_fusion.refs_0_), channel_id=1, source_target_pairs={{8,72},{24,88},{40,104},{56,120},{72,8},{88,24},{104,40},{120,56},... | collective-permute-start | bytes 786440 | tf_op jit(solution)/shard_map/ppermute | solution.py:236
  49.7 9.2 %collective-permute-start.13 = (f32[4,2,8,8,128]{4,3,2,1,0:T(8,128)S(1)}, f32[4,2,8,8,128]{4,3,2,1,0:T(8,128)S(1)}, u32[]{:S(2)}, u32[]{:S(2)}) collective-permute-start(f32[4,2,8,8,128]{4,3,2,1,0:T(8,128)S(1)} %add_add_fusion.refs_0_), channel_id=1, source_target_pairs={{8,0},{24,16},{40,32},{56,48},{72,64},{88,80},{104,96},{120,112},{... | collective-permute-start | bytes 786440 | tf_op jit(solution)/shard_map/ppermute | solution.py:240
  51.0 9.3 %collective-permute-start.12 = (f32[4,2,8,8,128]{4,3,2,1,0:T(8,128)S(1)}, f32[4,2,8,8,128]{4,3,2,1,0:T(8,128)S(1)}, u32[]{:S(2)}, u32[]{:S(2)}) collective-permute-start(f32[4,2,8,8,128]{4,3,2,1,0:T(8,128)S(1)} %add_add_fusion.refs_0_), channel_id=1, source_target_pairs={{8,24},{24,8},{40,56},{56,40},{72,88},{88,72},{104,120},{120,104},... | collective-permute-start | bytes 786440 | tf_op jit(solution)/shard_map/ppermute | solution.py:236
  55.0 6.6 %collective-permute-start.24 = (f32[4,2,8,8,128]{4,3,2,1,0:T(8,128)S(1)}, f32[4,2,8,8,128]{4,3,2,1,0:T(8,128)S(1)}, u32[]{:S(2)}, u32[]{:S(2)}) collective-permute-start(f32[4,2,8,8,128]{4,3,2,1,0:T(8,128)S(1)} %collective-permute-done.17.refs_4_), channel_id=1, source_target_pairs={{8,0},{24,16},{40,32},{56,48},{72,64},{88,80},{104,96},{120,112},{... | collective-permute-start | bytes 786440 | tf_op jit(solution)/shard_map/ppermute | solution.py:240
  56.3 9.2 %collective-permute-start.18 = (f32[4,2,8,8,128]{4,3,2,1,0:T(8,128)S(1)}, f32[4,2,8,8,128]{4,3,2,1,0:T(8,128)S(1)}, u32[]{:S(2)}, u32[]{:S(2)}) collective-permute-start(f32[4,2,8,8,128]{4,3,2,1,0:T(8,128)S(1)} %collective-permute-done.17.refs_4_), channel_id=1, source_target_pairs={{8,24},{24,8},{40,56},{56,40},{72,88},{88,72},{104,120},{120,104},... | collective-permute-start | bytes 786440 | tf_op jit(solution)/shard_map/ppermute | solution.py:236
  58.9 8.5 %collective-permute-start.19 = (f32[4,2,8,8,128]{4,3,2,1,0:T(8,128)S(1)}, f32[4,2,8,8,128]{4,3,2,1,0:T(8,128)S(1)}, u32[]{:S(2)}, u32[]{:S(2)}) collective-permute-start(f32[4,2,8,8,128]{4,3,2,1,0:T(8,128)S(1)} %collective-permute-done.13.refs_8_), channel_id=1, source_target_pairs={{0,96},{16,112},{32,64},{48,80},{64,32},{80,48},{96,0},{112,16},{1... | collective-permute-start | bytes 786440 | tf_op jit(solution)/shard_map/ppermute | solution.py:236
  59.6 9.1 %collective-permute-start.14 = (f32[4,2,8,8,128]{4,3,2,1,0:T(8,128)S(1)}, f32[4,2,8,8,128]{4,3,2,1,0:T(8,128)S(1)}, u32[]{:S(2)}, u32[]{:S(2)}) collective-permute-start(f32[4,2,8,8,128]{4,3,2,1,0:T(8,128)S(1)} %collective-permute-done.13.refs_8_), channel_id=1, source_target_pairs={{0,32},{16,48},{32,0},{48,16},{64,96},{80,112},{96,64},{112,80},{1... | collective-permute-start | bytes 786440 | tf_op jit(solution)/shard_map/ppermute | solution.py:236
  60.3 9.7 %collective-permute-start.22 = (f32[4,2,8,8,128]{4,3,2,1,0:T(8,128)S(1)}, f32[4,2,8,8,128]{4,3,2,1,0:T(8,128)S(1)}, u32[]{:S(2)}, u32[]{:S(2)}) collective-permute-start(f32[4,2,8,8,128]{4,3,2,1,0:T(8,128)S(1)} %collective-permute-done.12.refs_1_), channel_id=1, source_target_pairs={{8,0},{24,16},{40,32},{56,48},{72,64},{88,80},{104,96},{120,112},{... | collective-permute-start | bytes 786440 | tf_op jit(solution)/shard_map/ppermute | solution.py:240
  61.6 9.7 %collective-permute-start.21 = (f32[4,2,8,8,128]{4,3,2,1,0:T(8,128)S(1)}, f32[4,2,8,8,128]{4,3,2,1,0:T(8,128)S(1)}, u32[]{:S(2)}, u32[]{:S(2)}) collective-permute-start(f32[4,2,8,8,128]{4,3,2,1,0:T(8,128)S(1)} %collective-permute-done.12.refs_1_), channel_id=1, source_target_pairs={{8,104},{24,120},{40,72},{56,88},{72,40},{88,56},{104,8},{120,24},... | collective-permute-start | bytes 786440 | tf_op jit(solution)/shard_map/ppermute | solution.py:236
  65.5 9.0 %collective-permute-start.16 = (f32[4,2,8,8,128]{4,3,2,1,0:T(8,128)S(1)}, f32[4,2,8,8,128]{4,3,2,1,0:T(8,128)S(1)}, u32[]{:S(2)}, u32[]{:S(2)}) collective-permute-start(f32[4,2,8,8,128]{4,3,2,1,0:T(8,128)S(1)} %collective-permute-done.12.refs_1_), channel_id=1, source_target_pairs={{8,40},{24,56},{40,8},{56,24},{72,104},{88,120},{104,72},{120,88},... | collective-permute-start | bytes 786440 | tf_op jit(solution)/shard_map/ppermute | solution.py:236
  67.4 8.4 %collective-permute-start.25 = (f32[4,2,8,8,128]{4,3,2,1,0:T(8,128)S(1)}, f32[4,2,8,8,128]{4,3,2,1,0:T(8,128)S(1)}, u32[]{:S(2)}, u32[]{:S(2)}) collective-permute-start(f32[4,2,8,8,128]{4,3,2,1,0:T(8,128)S(1)} %collective-permute-done.18.refs_5_), channel_id=1, source_target_pairs={{8,0},{24,16},{40,32},{56,48},{72,64},{88,80},{104,96},{120,112},{... | collective-permute-start | bytes 786440 | tf_op jit(solution)/shard_map/ppermute | solution.py:240
  68.7 7.0 %collective-permute-start.20 = (f32[4,2,8,8,128]{4,3,2,1,0:T(8,128)S(1)}, f32[4,2,8,8,128]{4,3,2,1,0:T(8,128)S(1)}, u32[]{:S(2)}, u32[]{:S(2)}) collective-permute-start(f32[4,2,8,8,128]{4,3,2,1,0:T(8,128)S(1)} %collective-permute-done.19.refs_14_), channel_id=1, source_target_pairs={{0,8},{16,24},{32,40},{48,56},{64,72},{80,88},{96,104},{112,120},{... | collective-permute-start | bytes 786440 | tf_op jit(solution)/shard_map/ppermute | solution.py:240
  70.0 5.7 %collective-permute-start.15 = (f32[4,2,8,8,128]{4,3,2,1,0:T(8,128)S(1)}, f32[4,2,8,8,128]{4,3,2,1,0:T(8,128)S(1)}, u32[]{:S(2)}, u32[]{:S(2)}) collective-permute-start(f32[4,2,8,8,128]{4,3,2,1,0:T(8,128)S(1)} %collective-permute-done.14.refs_10_), channel_id=1, source_target_pairs={{0,8},{16,24},{32,40},{48,56},{64,72},{80,88},{96,104},{112,120},{... | collective-permute-start | bytes 786440 | tf_op jit(solution)/shard_map/ppermute | solution.py:240
  71.4 4.4 %collective-permute-start.26 = (f32[4,2,8,8,128]{4,3,2,1,0:T(8,128)S(1)}, f32[4,2,8,8,128]{4,3,2,1,0:T(8,128)S(1)}, u32[]{:S(2)}, u32[]{:S(2)}) collective-permute-start(f32[4,2,8,8,128]{4,3,2,1,0:T(8,128)S(1)} %collective-permute-done.21.refs_7_), channel_id=1, source_target_pairs={{8,0},{24,16},{40,32},{56,48},{72,64},{88,80},{104,96},{120,112},{... | collective-permute-start | bytes 786440 | tf_op jit(solution)/shard_map/ppermute | solution.py:240
  74.4 2.4 %collective-permute-start.23 = (f32[4,2,8,8,128]{4,3,2,1,0:T(8,128)S(1)}, f32[4,2,8,8,128]{4,3,2,1,0:T(8,128)S(1)}, u32[]{:S(2)}, u32[]{:S(2)}) collective-permute-start(f32[4,2,8,8,128]{4,3,2,1,0:T(8,128)S(1)} %collective-permute-done.16.refs_3_), channel_id=1, source_target_pairs={{8,0},{24,16},{40,32},{56,48},{72,64},{88,80},{104,96},{120,112},{... | collective-permute-start | bytes 786440 | tf_op jit(solution)/shard_map/ppermute | solution.py:240

commit v3 on v2

--- a/solution.py
+++ b/solution.py
@@ -196,21 +196,31 @@
     inside = (sublane < jnp.right_shift(8, short[4])) & (lane < jnp.right_shift(128, short[5]))
     tile = jnp.where(inside, 1.0, 0.0)
     by_d = [jnp.where(d < jnp.right_shift(8, short[3]), tile, 0.0) for d in range(8)]
-    copies = []
-    for row in range(4):
-        held_a = jnp.where(lax.rem(jnp.int32(row), spacing) == 0, 1.0, 0.0)
-        for slot in range(8):
-            for half in range(2):
-                at = (here ^ slot) * 2 + half
-                b, c = jnp.right_shift(at, 2), at & 3
-                held = jnp.where(
-                    (b < jnp.right_shift(4, short[1])) & (c < jnp.right_shift(4, short[2])), held_a, 0.0
-                )
-                for d in range(8):
-                    value = north[slot][row, half, d] + south[slot][row, half, d]
-                    scratch[row, at, d] = value * (by_d[d] * held)
-        copies.append(pltpu.make_async_copy(scratch.at[row], out.at[row], sems.at[row]))
-        copies[-1].start()
+    core = lax.axis_index("grid") & 1
+    copies = [pltpu.make_async_copy(scratch.at[row], out.at[row], sems.at[row]) for row in range(4)]
+
+    def write(pieces):
+        for row in range(4):
+            held_a = jnp.where(lax.rem(jnp.int32(row), spacing) == 0, 1.0, 0.0)
+            for slot, piece in enumerate(pieces):
+                for half in range(2):
+                    at = (here ^ slot) * 2 + half
+                    b, c = jnp.right_shift(at, 2), at & 3
+                    held = jnp.where(
+                        (b < jnp.right_shift(4, short[1])) & (c < jnp.right_shift(4, short[2])), held_a, 0.0
+                    )
+                    for d in range(8):
+                        scratch[row, at, d] = piece[row, half, d] * (by_d[d] * held)
+            copies[row].start()
+
+    @pl.when(core == 1)
+    def _():
+        write(north)
+
+    @pl.when(core == 0)
+    def _():
+        write(south)
+
     for copy in copies:
         copy.wait()
 
@@ -233,11 +243,8 @@
 
 
 def between(x, bits, cores):
-    return lax.ppermute(x, "grid", [(h * 2 + core, (h ^ bits) * 2 + core) for h in range(8) for core in cores])
-
-
-def across(x, core):
-    return lax.ppermute(x, "grid", [(h * 2 + core, h * 2 + 1 - core) for h in range(8)])
+    pairs = [(h * 2 + core, (h ^ bits if core in cores else h) * 2 + core) for h in range(8) for core in range(2)]
+    return lax.ppermute(x, "grid", pairs)
 
 
 def to_previous(x, bits):
@@ -257,13 +264,13 @@
     for_y2 = lax.optimization_barrier(parts[3]) + between(parts[0], 1, (1,))
     arrived = between(parts[1], 2, (0, 1))
     arrived = arrived + between(parts[2], 6, (0, 1))
-    own_z = across(parts[0], 0)
+    own_z = swap(parts[0], 1)
     share = between(for_y2, 4, (1,))
     share = share + between(own_z + arrived, 1, (1,))
-    share = share + across(parts[3] + arrived, 0)
+    share = share + swap(parts[3] + arrived, 1)
     north, south = {0: share}, {}
     north[1] = between(share, 1, (1,))
-    south[0] = across(share, 1)
+    south[0] = swap(share, 1)
     north[4] = between(share, 4, (1,))
     south[2] = between(south[0], 2, (0,))
     south[6] = between(south[0], 6, (0,))
@@ -271,9 +278,9 @@
     north[7] = between(north[1], 6, (1,))
     north[5] = between(north[4], 1, (1,))
     for slot in (1, 4, 3, 7, 5):
-        south[slot] = across(north[slot], 1)
+        south[slot] = swap(north[slot], 1)
     for slot in (2, 6):
-        north[slot] = across(south[slot], 0)
+        north[slot] = swap(south[slot], 1)
     return restrict(levels, [north[slot] for slot in range(8)] + [south[slot] for slot in range(8)])
 
 

time: 79.7 us -> 75.1 us (0.942)
  starting transfers between devices: 50.5 us -> 41.6 us
  waiting for transfers between devices: 20 us -> 24.7 us
    ppermute x22 -> x12, starting transfers between devices: 42.3 us -> 27.6 us  [between(): return lax.ppermute(x, 'grid', pairs)]
    ppermute x3 -> x13, starting transfers between devices: 2.29 us -> 8.11 us  [swap(): return lax.ppermute(x, 'grid', [(i, i ^ bits) for i in range(16)])]
    ppermute x22 -> x12, waiting for transfers between devices: 9.69 us -> 12.9 us  [between(): return lax.ppermute(x, 'grid', pairs)]
    ppermute x3 -> x13, waiting for transfers between devices: 0.82 us -> 2.36 us  [swap(): return lax.ppermute(x, 'grid', [(i, i ^ bits) for i in range(16)])]
  transfers between devices with their start and end apart: 27 -> 27, of which waited for: 7 -> 10; matrix products, arithmetic and copies ran while one was open for 0% -> 0% of each run, Pallas kernels for 0% -> 0%
where the time goes in v3:
time: 75.1 us; the launch traced here: 74.7 us
  starting transfers between devices  41.6 us (55%)
  waiting for transfers between devices  24.7 us (33%)
  Pallas kernels  7.39 us (10%)
  between operations  0.86 us (1%)
    ppermute x12, starting transfers between devices, between(): return lax.ppermute(x, 'grid', pairs)  27.6 us
    ppermute x12, waiting for transfers between devices, between(): return lax.ppermute(x, 'grid', pairs)  12.9 us
    ppermute x2, waiting for transfers between devices, to_previous(): return lax.ppermute(x, ('grid', 'dom'), pairs)  9.48 us
    ppermute x13, starting transfers between devices, swap(): return lax.ppermute(x, 'grid', [(i, i ^ bits) for i in range(16)])  8.11 us
    ppermute x2, starting transfers between devices, to_previous(): return lax.ppermute(x, ('grid', 'dom'), pairs)  5.87 us
    pallas_call x2, Pallas kernels, interp_rows(): pl.pallas_call(interp_kernel, grid=(count,), in_specs=[smem, smem, pl.Blo...  4.51 us
    ppermute x13, waiting for transfers between devices, swap(): return lax.ppermute(x, 'grid', [(i, i ^ bits) for i in range(16)])  2.36 us
    pallas_call x1, Pallas kernels, restrict(): pl.pallas_call(restrict_kernel, in_specs=[pl.BlockSpec(memory_space=pltpu...  2.1 us
  transfers between devices with their start and end apart: 27, of which 10 were waited for; matrix products, arithmetic and copies ran while one was open for 0% of the time, Pallas kernels for 0%

profile of v3, /device:TPU:1, one launch (start us, length us, event | category | flops | bytes accessed | tf_op | source)
XLA Modules:
  0.0 74.7 jit_solution(1405646954911697397)
XLA Ops:
  0.7 1.5 %shard_map.46 = (f32[4,1,2,8,8,128]{5,4,3,2,1,0:T(8,128)S(1)}, f32[4,1,2,8,8,128]{5,4,3,2,1,0:T(8,128)S(1)}) custom-call(s32[1,6]{1,0:T(1,128)} %levels.7, s32[1]{0:T(128)S(6)} %copy.5.coefs, f32[1,4,4,4,8,8,128]{6,5,4,3,2,1,0:T(8,128)} %x.3, bf16[3,128,128]{2,1,0:T(8,128)(2,1)} %constant.2.clone.pf), custom_call_target="tpu_custom_call" | custom-call | flops 100000000 | bytes 1048576 | tf_op jit(solution)/shard_map/pallas_call | solution.py:136
  2.1 3.1 %shard_map.47 = (f32[4,3,2,8,8,128]{5,4,3,2,1,0:T(8,128)S(1)}, f32[4,3,2,8,8,128]{5,4,3,2,1,0:T(8,128)S(1)}) custom-call(s32[1,6]{1,0:T(1,128)} %levels.7, s32[1]{0:T(128)S(6)} %copy.5.coefs, f32[1,4,4,4,8,8,128]{6,5,4,3,2,1,0:T(8,128)} %x.3, bf16[3,128,128]{2,1,0:T(8,128)(2,1)} %constant.2.clone.pf, f32[4,1,2,8,8,128]{5,4,3,2,1,0:T(8,128)S(1)} %get-tuple-element.13.rest_0_.own0), custom_call_target="tpu_custom_call" | custom-call | flops 300000000 | bytes 3145728 | tf_op jit(solution)/shard_map/pallas_call | solution.py:136
  5.2 1.5 %collective-permute-start.2 = (f32[4,3,2,8,8,128]{5,4,3,2,1,0:T(8,128)S(1)}, f32[4,3,2,8,8,128]{5,4,3,2,1,0:T(8,128)S(1)}, u32[]{:S(2)}, u32[]{:S(2)}) collective-permute-start(f32[4,3,2,8,8,128]{5,4,3,2,1,0:T(8,128)S(1)} %get-tuple-element.16), channel_id=1, source_target_pairs={{0,8},{8,0},{16,24},{24,16},{32,40},{40,32},{48,56},{56,48},{64,72... | collective-permute-start | bytes 2359304 | tf_op jit(solution)/shard_map/ppermute | solution.py:242
  6.7 5.9 %collective-permute-start.4 = (f32[4,1,2,8,8,128]{5,4,3,2,1,0:T(8,128)S(1)}, f32[4,1,2,8,8,128]{5,4,3,2,1,0:T(8,128)S(1)}, u32[]{:S(2)}, u32[]{:S(2)}) collective-permute-start(f32[4,1,2,8,8,128]{5,4,3,2,1,0:T(8,128)S(1)} %get-tuple-element.15), channel_id=1, source_target_pairs={{0,15},{1,8},{2,9},{3,10},{4,11},{5,12},{6,13},{7,14},{8,7},{9,0},... | collective-permute-start | bytes 786440 | tf_op jit(solution)/shard_map/ppermute | solution.py:252
  12.5 0.4 collective-permute-start.1
  13.4 0.8 %collective-permute-done.others = s32[1,6]{1,0:T(1,128)S(1)} collective-permute-done((s32[1,6]{1,0:T(1,128)S(1)}, s32[1,6]{1,0:T(1,128)S(1)}, u32[]{:S(2)}, u32[]{:S(2)}) %collective-permute-start) | collective-permute-done | bytes 56 | tf_op jit(solution)/shard_map/ppermute | solution.py:242
  14.2 3.9 %collective-permute-done.4.next_got = f32[4,1,2,8,8,128]{5,4,3,2,1,0:T(8,128)S(1)} collective-permute-done((f32[4,1,2,8,8,128]{5,4,3,2,1,0:T(8,128)S(1)}, f32[4,1,2,8,8,128]{5,4,3,2,1,0:T(8,128)S(1)}, u32[]{:S(2)}, u32[]{:S(2)}) %collective-permute-start.4) | collective-permute-done | bytes 262176 | tf_op jit(solution)/shard_map/ppermute | solution.py:252
  18.0 5.6 %collective-permute-done.3.next_own = f32[4,1,2,8,8,128]{5,4,3,2,1,0:T(8,128)S(1)} collective-permute-done((f32[4,1,2,8,8,128]{5,4,3,2,1,0:T(8,128)S(1)}, f32[4,1,2,8,8,128]{5,4,3,2,1,0:T(8,128)S(1)}, u32[]{:S(2)}, u32[]{:S(2)}) %collective-permute-start.3) | collective-permute-done | bytes 262176 | tf_op jit(solution)/shard_map/ppermute | solution.py:252
  23.7 0.8 %combine.1 = (f32[4,2,8,8,128]{4,3,2,1,0:T(8,128)S(1)}, f32[4,2,8,8,128]{4,3,2,1,0:T(8,128)S(1)}, f32[4,2,8,8,128]{4,3,2,1,0:T(8,128)S(1)}, f32[4,2,8,8,128]{4,3,2,1,0:T(8,128)S(1)}) custom-call(s32[1,6]{1,0:T(1,128)S(1)} %copy-done, s32[1,6]{1,0:T(1,128)S(1)} %collective-permute-done.others, f32[4,1,2,8,8,128]{5,4,3,2,1,0:T(8,128)S(1)} %get-tuple-element.13.rest_0_.own0, ...), custom_call_target="tpu_custom_call" | custom-call | tf_op jit(solution)/shard_map/combine/pallas_call | solution.py:179
  24.4 1.4 %collective-permute-start.8 = (f32[4,2,8,8,128]{4,3,2,1,0:T(8,128)S(1)}, f32[4,2,8,8,128]{4,3,2,1,0:T(8,128)S(1)}, u32[]{:S(2)}, u32[]{:S(2)}) collective-permute-start(f32[4,2,8,8,128]{4,3,2,1,0:T(8,128)S(1)} %get-tuple-element.19), channel_id=1, source_target_pairs={{0,32},{8,40},{16,48},{24,56},{32,0},{40,8},{48,16},{56,24},{64,96... | collective-permute-start | bytes 786440 | tf_op jit(solution)/shard_map/ppermute | solution.py:247
  25.8 1.9 %collective-permute-start.9 = (f32[4,2,8,8,128]{4,3,2,1,0:T(8,128)S(1)}, f32[4,2,8,8,128]{4,3,2,1,0:T(8,128)S(1)}, u32[]{:S(2)}, u32[]{:S(2)}) collective-permute-start(f32[4,2,8,8,128]{4,3,2,1,0:T(8,128)S(1)} %get-tuple-element.20), channel_id=1, source_target_pairs={{0,96},{8,104},{16,112},{24,120},{32,64},{40,72},{48,80},{56,88},{... | collective-permute-start | bytes 786440 | tf_op jit(solution)/shard_map/ppermute | solution.py:247
  27.7 1.6 %collective-permute-start.7 = (f32[4,2,8,8,128]{4,3,2,1,0:T(8,128)S(1)}, f32[4,2,8,8,128]{4,3,2,1,0:T(8,128)S(1)}, u32[]{:S(2)}, u32[]{:S(2)}) collective-permute-start(f32[4,2,8,8,128]{4,3,2,1,0:T(8,128)S(1)} %get-tuple-element.18), channel_id=1, source_target_pairs={{0,8},{8,0},{16,24},{24,16},{32,40},{40,32},{48,56},{56,48},{64,72... | collective-permute-start | bytes 786440 | tf_op jit(solution)/shard_map/ppermute | solution.py:242
  29.3 2.7 %collective-permute-start.5 = (f32[4,2,8,8,128]{4,3,2,1,0:T(8,128)S(1)}, f32[4,2,8,8,128]{4,3,2,1,0:T(8,128)S(1)}, u32[]{:S(2)}, u32[]{:S(2)}) collective-permute-start(f32[4,2,8,8,128]{4,3,2,1,0:T(8,128)S(1)} %get-tuple-element.18), channel_id=1, source_target_pairs={{0,0},{8,24},{16,16},{24,8},{32,32},{40,56},{48,48},{56,40},{64,64... | collective-permute-start | bytes 786440 | tf_op jit(solution)/shard_map/ppermute | solution.py:247
  31.9 1.7 %collective-permute-done.9 = f32[4,2,8,8,128]{4,3,2,1,0:T(8,128)S(1)} collective-permute-done((f32[4,2,8,8,128]{4,3,2,1,0:T(8,128)S(1)}, f32[4,2,8,8,128]{4,3,2,1,0:T(8,128)S(1)}, u32[]{:S(2)}, u32[]{:S(2)}) %collective-permute-start.9) | collective-permute-done | bytes 262176 | tf_op jit(solution)/shard_map/ppermute | solution.py:247
  33.7 2.7 %collective-permute-start.10 = (f32[4,2,8,8,128]{4,3,2,1,0:T(8,128)S(1)}, f32[4,2,8,8,128]{4,3,2,1,0:T(8,128)S(1)}, u32[]{:S(2)}, u32[]{:S(2)}) collective-permute-start(f32[4,2,8,8,128]{4,3,2,1,0:T(8,128)S(1)} %get-tuple-element.21), channel_id=1, source_target_pairs={{0,0},{8,24},{16,16},{24,8},{32,32},{40,56},{48,48},{56,40},{64,64... | collective-permute-start | bytes 786440 | tf_op jit(solution)/shard_map/ppermute | solution.py:247
  36.6 3.3 %collective-permute-start.6 = (f32[4,2,8,8,128]{4,3,2,1,0:T(8,128)S(1)}, f32[4,2,8,8,128]{4,3,2,1,0:T(8,128)S(1)}, u32[]{:S(2)}, u32[]{:S(2)}) collective-permute-start(f32[4,2,8,8,128]{4,3,2,1,0:T(8,128)S(1)} %add.18), channel_id=1, source_target_pairs={{0,0},{8,72},{16,16},{24,88},{32,32},{40,104},{48,48},{56,120},{64... | collective-permute-start | bytes 786440 | tf_op jit(solution)/shard_map/ppermute | solution.py:247
  40.0 0.8 %collective-permute-done.10 = f32[4,2,8,8,128]{4,3,2,1,0:T(8,128)S(1)} collective-permute-done((f32[4,2,8,8,128]{4,3,2,1,0:T(8,128)S(1)}, f32[4,2,8,8,128]{4,3,2,1,0:T(8,128)S(1)}, u32[]{:S(2)}, u32[]{:S(2)}) %collective-permute-start.10) | collective-permute-done | bytes 262176 | tf_op jit(solution)/shard_map/ppermute | solution.py:247
  40.8 4.4 %collective-permute-done.6 = f32[4,2,8,8,128]{4,3,2,1,0:T(8,128)S(1)} collective-permute-done((f32[4,2,8,8,128]{4,3,2,1,0:T(8,128)S(1)}, f32[4,2,8,8,128]{4,3,2,1,0:T(8,128)S(1)}, u32[]{:S(2)}, u32[]{:S(2)}) %collective-permute-start.6) | collective-permute-done | bytes 262176 | tf_op jit(solution)/shard_map/ppermute | solution.py:247
  45.3 3.3 %collective-permute-start.17 = (f32[4,2,8,8,128]{4,3,2,1,0:T(8,128)S(1)}, f32[4,2,8,8,128]{4,3,2,1,0:T(8,128)S(1)}, u32[]{:S(2)}, u32[]{:S(2)}) collective-permute-start(f32[4,2,8,8,128]{4,3,2,1,0:T(8,128)S(1)} %add_add_fusion.refs_0_), channel_id=1, source_target_pairs={{0,0},{8,72},{16,16},{24,88},{32,32},{40,104},{48,48},{56,120},{64... | collective-permute-start | bytes 786440 | tf_op jit(solution)/shard_map/ppermute | solution.py:247
  48.7 2.7 %collective-permute-start.12 = (f32[4,2,8,8,128]{4,3,2,1,0:T(8,128)S(1)}, f32[4,2,8,8,128]{4,3,2,1,0:T(8,128)S(1)}, u32[]{:S(2)}, u32[]{:S(2)}) collective-permute-start(f32[4,2,8,8,128]{4,3,2,1,0:T(8,128)S(1)} %add_add_fusion.refs_0_), channel_id=1, source_target_pairs={{0,0},{8,24},{16,16},{24,8},{32,32},{40,56},{48,48},{56,40},{64,64... | collective-permute-start | bytes 786440 | tf_op jit(solution)/shard_map/ppermute | solution.py:247
  51.4 2.5 %collective-permute-done.17.refs_4_ = f32[4,2,8,8,128]{4,3,2,1,0:T(8,128)S(1)} collective-permute-done((f32[4,2,8,8,128]{4,3,2,1,0:T(8,128)S(1)}, f32[4,2,8,8,128]{4,3,2,1,0:T(8,128)S(1)}, u32[]{:S(2)}, u32[]{:S(2)}) %collective-permute-start.17) | collective-permute-done | bytes 262176 | tf_op jit(solution)/shard_map/ppermute | solution.py:247
  53.9 2.6 %collective-permute-start.18 = (f32[4,2,8,8,128]{4,3,2,1,0:T(8,128)S(1)}, f32[4,2,8,8,128]{4,3,2,1,0:T(8,128)S(1)}, u32[]{:S(2)}, u32[]{:S(2)}) collective-permute-start(f32[4,2,8,8,128]{4,3,2,1,0:T(8,128)S(1)} %collective-permute-done.17.refs_4_), channel_id=1, source_target_pairs={{0,0},{8,24},{16,16},{24,8},{32,32},{40,56},{48,48},{56,40},{64,64... | collective-permute-start | bytes 786440 | tf_op jit(solution)/shard_map/ppermute | solution.py:247
  56.6 0.7 collective-permute-start.19
  57.3 0.7 collective-permute-start.14
  58.0 3.3 %collective-permute-start.22 = (f32[4,2,8,8,128]{4,3,2,1,0:T(8,128)S(1)}, f32[4,2,8,8,128]{4,3,2,1,0:T(8,128)S(1)}, u32[]{:S(2)}, u32[]{:S(2)}) collective-permute-start(f32[4,2,8,8,128]{4,3,2,1,0:T(8,128)S(1)} %collective-permute-done.12.refs_1_), channel_id=1, source_target_pairs={{0,8},{8,0},{16,24},{24,16},{32,40},{40,32},{48,56},{56,48},{64,72... | collective-permute-start | bytes 786440 | tf_op jit(solution)/shard_map/ppermute | solution.py:242
  61.2 2.7 %collective-permute-start.21 = (f32[4,2,8,8,128]{4,3,2,1,0:T(8,128)S(1)}, f32[4,2,8,8,128]{4,3,2,1,0:T(8,128)S(1)}, u32[]{:S(2)}, u32[]{:S(2)}) collective-permute-start(f32[4,2,8,8,128]{4,3,2,1,0:T(8,128)S(1)} %collective-permute-done.12.refs_1_), channel_id=1, source_target_pairs={{0,0},{8,104},{16,16},{24,120},{32,32},{40,72},{48,48},{56,88},{64... | collective-permute-start | bytes 786440 | tf_op jit(solution)/shard_map/ppermute | solution.py:247
  63.9 3.0 %collective-permute-start.16 = (f32[4,2,8,8,128]{4,3,2,1,0:T(8,128)S(1)}, f32[4,2,8,8,128]{4,3,2,1,0:T(8,128)S(1)}, u32[]{:S(2)}, u32[]{:S(2)}) collective-permute-start(f32[4,2,8,8,128]{4,3,2,1,0:T(8,128)S(1)} %collective-permute-done.12.refs_1_), channel_id=1, source_target_pairs={{0,0},{8,40},{16,16},{24,56},{32,32},{40,8},{48,48},{56,24},{64,64... | collective-permute-start | bytes 786440 | tf_op jit(solution)/shard_map/ppermute | solution.py:247
  67.1 0.5 collective-permute-start.20
  67.7 1.9 %collective-permute-done.21.refs_7_ = f32[4,2,8,8,128]{4,3,2,1,0:T(8,128)S(1)} collective-permute-done((f32[4,2,8,8,128]{4,3,2,1,0:T(8,128)S(1)}, f32[4,2,8,8,128]{4,3,2,1,0:T(8,128)S(1)}, u32[]{:S(2)}, u32[]{:S(2)}) %collective-permute-start.21) | collective-permute-done | bytes 262176 | tf_op jit(solution)/shard_map/ppermute | solution.py:247
  69.6 1.5 %collective-permute-done.16.refs_3_ = f32[4,2,8,8,128]{4,3,2,1,0:T(8,128)S(1)} collective-permute-done((f32[4,2,8,8,128]{4,3,2,1,0:T(8,128)S(1)}, f32[4,2,8,8,128]{4,3,2,1,0:T(8,128)S(1)}, u32[]{:S(2)}, u32[]{:S(2)}) %collective-permute-start.16) | collective-permute-done | bytes 262176 | tf_op jit(solution)/shard_map/ppermute | solution.py:247
  71.1 1.5 %collective-permute-done.23.refs_11_ = f32[4,2,8,8,128]{4,3,2,1,0:T(8,128)S(1)} collective-permute-done((f32[4,2,8,8,128]{4,3,2,1,0:T(8,128)S(1)}, f32[4,2,8,8,128]{4,3,2,1,0:T(8,128)S(1)}, u32[]{:S(2)}, u32[]{:S(2)}) %collective-permute-start.23) | collective-permute-done | bytes 262176 | tf_op jit(solution)/shard_map/ppermute | solution.py:242
  72.6 2.1 %restrict.1 = f32[4,16,8,8,128]{4,3,2,1,0:T(8,128)} custom-call(s32[1,6]{1,0:T(1,128)S(1)} %copy-done, f32[4,2,8,8,128]{4,3,2,1,0:T(8,128)S(1)} %add_add_fusion.refs_0_, f32[4,2,8,8,128]{4,3,2,1,0:T(8,128)S(1)} %collective-permute-done.12.refs_1_, f32[4,2,8,8,128]{4,3,2,1,0:T(8,128)S(1)} %collective-permute-done.15.refs_2_, ...), custom_call_target="tpu_custom_call" | custom-call | tf_op jit(solution)/shard_map/restrict/pallas_call | solution.py:229
  (31 shorter events, 1.1 us)
Async XLA Ops:
  0.7 12.3 %copy-start = (s32[1,6]{1,0:T(1,128)S(1)}, s32[1,6]{1,0:T(1,128)}, u32[]{:S(2)}) copy-start(s32[1,6]{1,0:T(1,128)} %levels.7) | copy-start | bytes 76
  5.2 18.5 %collective-permute-start.2 = (f32[4,3,2,8,8,128]{5,4,3,2,1,0:T(8,128)S(1)}, f32[4,3,2,8,8,128]{5,4,3,2,1,0:T(8,128)S(1)}, u32[]{:S(2)}, u32[]{:S(2)}) collective-permute-start(f32[4,3,2,8,8,128]{5,4,3,2,1,0:T(8,128)S(1)} %get-tuple-element.16), channel_id=1, source_target_pairs={{0,8},{8,0},{16,24},{24,16},{32,40},{40,32},{48,56},{56,48},{64,72... | collective-permute-start | bytes 2359304 | tf_op jit(solution)/shard_map/ppermute | solution.py:242
  6.7 11.4 %collective-permute-start.4 = (f32[4,1,2,8,8,128]{5,4,3,2,1,0:T(8,128)S(1)}, f32[4,1,2,8,8,128]{5,4,3,2,1,0:T(8,128)S(1)}, u32[]{:S(2)}, u32[]{:S(2)}) collective-permute-start(f32[4,1,2,8,8,128]{5,4,3,2,1,0:T(8,128)S(1)} %get-tuple-element.15), channel_id=1, source_target_pairs={{0,15},{1,8},{2,9},{3,10},{4,11},{5,12},{6,13},{7,14},{8,7},{9,0},... | collective-permute-start | bytes 786440 | tf_op jit(solution)/shard_map/ppermute | solution.py:252
  12.5 5.5 %collective-permute-start.1 = (f32[4,1,2,8,8,128]{5,4,3,2,1,0:T(8,128)S(1)}, f32[4,1,2,8,8,128]{5,4,3,2,1,0:T(8,128)S(1)}, u32[]{:S(2)}, u32[]{:S(2)}) collective-permute-start(f32[4,1,2,8,8,128]{5,4,3,2,1,0:T(8,128)S(1)} %get-tuple-element.15), channel_id=1, source_target_pairs={{0,8},{8,0},{16,24},{24,16},{32,40},{40,32},{48,56},{56,48},{64,72... | collective-permute-start | bytes 786440 | tf_op jit(solution)/shard_map/ppermute | solution.py:242
  13.0 10.7 %collective-permute-start.3 = (f32[4,1,2,8,8,128]{5,4,3,2,1,0:T(8,128)S(1)}, f32[4,1,2,8,8,128]{5,4,3,2,1,0:T(8,128)S(1)}, u32[]{:S(2)}, u32[]{:S(2)}) collective-permute-start(f32[4,1,2,8,8,128]{5,4,3,2,1,0:T(8,128)S(1)} %get-tuple-element.13.rest_0_.own0), channel_id=1, source_target_pairs={{0,7},{1,0},{2,1},{3,2},{4,3},{5,4},{6,5},{7,6},{8,15},{9,8},{10,9... | collective-permute-start | bytes 786440 | tf_op jit(solution)/shard_map/ppermute | solution.py:252
  13.0 1.2 %collective-permute-start = (s32[1,6]{1,0:T(1,128)S(1)}, s32[1,6]{1,0:T(1,128)S(1)}, u32[]{:S(2)}, u32[]{:S(2)}) collective-permute-start(s32[1,6]{1,0:T(1,128)S(1)} %copy-done), channel_id=1, source_target_pairs={{0,8},{8,0},{16,24},{24,16},{32,40},{40,32},{48,56},{56,48},{64,72... | collective-permute-start | bytes 80 | tf_op jit(solution)/shard_map/ppermute | solution.py:242
  24.4 7.5 %collective-permute-start.8 = (f32[4,2,8,8,128]{4,3,2,1,0:T(8,128)S(1)}, f32[4,2,8,8,128]{4,3,2,1,0:T(8,128)S(1)}, u32[]{:S(2)}, u32[]{:S(2)}) collective-permute-start(f32[4,2,8,8,128]{4,3,2,1,0:T(8,128)S(1)} %get-tuple-element.19), channel_id=1, source_target_pairs={{0,32},{8,40},{16,48},{24,56},{32,0},{40,8},{48,16},{56,24},{64,96... | collective-permute-start | bytes 786440 | tf_op jit(solution)/shard_map/ppermute | solution.py:247
  25.8 7.8 %collective-permute-start.9 = (f32[4,2,8,8,128]{4,3,2,1,0:T(8,128)S(1)}, f32[4,2,8,8,128]{4,3,2,1,0:T(8,128)S(1)}, u32[]{:S(2)}, u32[]{:S(2)}) collective-permute-start(f32[4,2,8,8,128]{4,3,2,1,0:T(8,128)S(1)} %get-tuple-element.20), channel_id=1, source_target_pairs={{0,96},{8,104},{16,112},{24,120},{32,64},{40,72},{48,80},{56,88},{... | collective-permute-start | bytes 786440 | tf_op jit(solution)/shard_map/ppermute | solution.py:247
  27.7 5.9 %collective-permute-start.7 = (f32[4,2,8,8,128]{4,3,2,1,0:T(8,128)S(1)}, f32[4,2,8,8,128]{4,3,2,1,0:T(8,128)S(1)}, u32[]{:S(2)}, u32[]{:S(2)}) collective-permute-start(f32[4,2,8,8,128]{4,3,2,1,0:T(8,128)S(1)} %get-tuple-element.18), channel_id=1, source_target_pairs={{0,8},{8,0},{16,24},{24,16},{32,40},{40,32},{48,56},{56,48},{64,72... | collective-permute-start | bytes 786440 | tf_op jit(solution)/shard_map/ppermute | solution.py:242
  29.3 7.3 %collective-permute-start.5 = (f32[4,2,8,8,128]{4,3,2,1,0:T(8,128)S(1)}, f32[4,2,8,8,128]{4,3,2,1,0:T(8,128)S(1)}, u32[]{:S(2)}, u32[]{:S(2)}) collective-permute-start(f32[4,2,8,8,128]{4,3,2,1,0:T(8,128)S(1)} %get-tuple-element.18), channel_id=1, source_target_pairs={{0,0},{8,24},{16,16},{24,8},{32,32},{40,56},{48,48},{56,40},{64,64... | collective-permute-start | bytes 786440 | tf_op jit(solution)/shard_map/ppermute | solution.py:247
  33.7 7.1 %collective-permute-start.10 = (f32[4,2,8,8,128]{4,3,2,1,0:T(8,128)S(1)}, f32[4,2,8,8,128]{4,3,2,1,0:T(8,128)S(1)}, u32[]{:S(2)}, u32[]{:S(2)}) collective-permute-start(f32[4,2,8,8,128]{4,3,2,1,0:T(8,128)S(1)} %get-tuple-element.21), channel_id=1, source_target_pairs={{0,0},{8,24},{16,16},{24,8},{32,32},{40,56},{48,48},{56,40},{64,64... | collective-permute-start | bytes 786440 | tf_op jit(solution)/shard_map/ppermute | solution.py:247
  36.4 4.5 %collective-permute-start.11 = (f32[4,2,8,8,128]{4,3,2,1,0:T(8,128)S(1)}, f32[4,2,8,8,128]{4,3,2,1,0:T(8,128)S(1)}, u32[]{:S(2)}, u32[]{:S(2)}) collective-permute-start(f32[4,2,8,8,128]{4,3,2,1,0:T(8,128)S(1)} %get-tuple-element.22), channel_id=1, source_target_pairs={{0,8},{8,0},{16,24},{24,16},{32,40},{40,32},{48,56},{56,48},{64,72... | collective-permute-start | bytes 786440 | tf_op jit(solution)/shard_map/ppermute | solution.py:242
  36.6 8.6 %collective-permute-start.6 = (f32[4,2,8,8,128]{4,3,2,1,0:T(8,128)S(1)}, f32[4,2,8,8,128]{4,3,2,1,0:T(8,128)S(1)}, u32[]{:S(2)}, u32[]{:S(2)}) collective-permute-start(f32[4,2,8,8,128]{4,3,2,1,0:T(8,128)S(1)} %add.18), channel_id=1, source_target_pairs={{0,0},{8,72},{16,16},{24,88},{32,32},{40,104},{48,48},{56,120},{64... | collective-permute-start | bytes 786440 | tf_op jit(solution)/shard_map/ppermute | solution.py:247
  45.3 8.6 %collective-permute-start.17 = (f32[4,2,8,8,128]{4,3,2,1,0:T(8,128)S(1)}, f32[4,2,8,8,128]{4,3,2,1,0:T(8,128)S(1)}, u32[]{:S(2)}, u32[]{:S(2)}) collective-permute-start(f32[4,2,8,8,128]{4,3,2,1,0:T(8,128)S(1)} %add_add_fusion.refs_0_), channel_id=1, source_target_pairs={{0,0},{8,72},{16,16},{24,88},{32,32},{40,104},{48,48},{56,120},{64... | collective-permute-start | bytes 786440 | tf_op jit(solution)/shard_map/ppermute | solution.py:247
  48.6 8.0 %collective-permute-start.13 = (f32[4,2,8,8,128]{4,3,2,1,0:T(8,128)S(1)}, f32[4,2,8,8,128]{4,3,2,1,0:T(8,128)S(1)}, u32[]{:S(2)}, u32[]{:S(2)}) collective-permute-start(f32[4,2,8,8,128]{4,3,2,1,0:T(8,128)S(1)} %add_add_fusion.refs_0_), channel_id=1, source_target_pairs={{0,8},{8,0},{16,24},{24,16},{32,40},{40,32},{48,56},{56,48},{64,72... | collective-permute-start | bytes 786440 | tf_op jit(solution)/shard_map/ppermute | solution.py:242
  48.7 9.2 %collective-permute-start.12 = (f32[4,2,8,8,128]{4,3,2,1,0:T(8,128)S(1)}, f32[4,2,8,8,128]{4,3,2,1,0:T(8,128)S(1)}, u32[]{:S(2)}, u32[]{:S(2)}) collective-permute-start(f32[4,2,8,8,128]{4,3,2,1,0:T(8,128)S(1)} %add_add_fusion.refs_0_), channel_id=1, source_target_pairs={{0,0},{8,24},{16,16},{24,8},{32,32},{40,56},{48,48},{56,40},{64,64... | collective-permute-start | bytes 786440 | tf_op jit(solution)/shard_map/ppermute | solution.py:247
  53.9 7.3 %collective-permute-start.24 = (f32[4,2,8,8,128]{4,3,2,1,0:T(8,128)S(1)}, f32[4,2,8,8,128]{4,3,2,1,0:T(8,128)S(1)}, u32[]{:S(2)}, u32[]{:S(2)}) collective-permute-start(f32[4,2,8,8,128]{4,3,2,1,0:T(8,128)S(1)} %collective-permute-done.17.refs_4_), channel_id=1, source_target_pairs={{0,8},{8,0},{16,24},{24,16},{32,40},{40,32},{48,56},{56,48},{64,72... | collective-permute-start | bytes 786440 | tf_op jit(solution)/shard_map/ppermute | solution.py:242
  53.9 10.0 %collective-permute-start.18 = (f32[4,2,8,8,128]{4,3,2,1,0:T(8,128)S(1)}, f32[4,2,8,8,128]{4,3,2,1,0:T(8,128)S(1)}, u32[]{:S(2)}, u32[]{:S(2)}) collective-permute-start(f32[4,2,8,8,128]{4,3,2,1,0:T(8,128)S(1)} %collective-permute-done.17.refs_4_), channel_id=1, source_target_pairs={{0,0},{8,24},{16,16},{24,8},{32,32},{40,56},{48,48},{56,40},{64,64... | collective-permute-start | bytes 786440 | tf_op jit(solution)/shard_map/ppermute | solution.py:247
  56.6 10.4 %collective-permute-start.19 = (f32[4,2,8,8,128]{4,3,2,1,0:T(8,128)S(1)}, f32[4,2,8,8,128]{4,3,2,1,0:T(8,128)S(1)}, u32[]{:S(2)}, u32[]{:S(2)}) collective-permute-start(f32[4,2,8,8,128]{4,3,2,1,0:T(8,128)S(1)} %collective-permute-done.13.refs_8_), channel_id=1, source_target_pairs={{0,96},{8,8},{16,112},{24,24},{32,64},{40,40},{48,80},{56,56},{64,... | collective-permute-start | bytes 786440 | tf_op jit(solution)/shard_map/ppermute | solution.py:247
  57.3 9.8 %collective-permute-start.14 = (f32[4,2,8,8,128]{4,3,2,1,0:T(8,128)S(1)}, f32[4,2,8,8,128]{4,3,2,1,0:T(8,128)S(1)}, u32[]{:S(2)}, u32[]{:S(2)}) collective-permute-start(f32[4,2,8,8,128]{4,3,2,1,0:T(8,128)S(1)} %collective-permute-done.13.refs_8_), channel_id=1, source_target_pairs={{0,32},{8,8},{16,48},{24,24},{32,0},{40,40},{48,16},{56,56},{64,96... | collective-permute-start | bytes 786440 | tf_op jit(solution)/shard_map/ppermute | solution.py:247
  58.0 9.6 %collective-permute-start.22 = (f32[4,2,8,8,128]{4,3,2,1,0:T(8,128)S(1)}, f32[4,2,8,8,128]{4,3,2,1,0:T(8,128)S(1)}, u32[]{:S(2)}, u32[]{:S(2)}) collective-permute-start(f32[4,2,8,8,128]{4,3,2,1,0:T(8,128)S(1)} %collective-permute-done.12.refs_1_), channel_id=1, source_target_pairs={{0,8},{8,0},{16,24},{24,16},{32,40},{40,32},{48,56},{56,48},{64,72... | collective-permute-start | bytes 786440 | tf_op jit(solution)/shard_map/ppermute | solution.py:242
  61.2 8.3 %collective-permute-start.21 = (f32[4,2,8,8,128]{4,3,2,1,0:T(8,128)S(1)}, f32[4,2,8,8,128]{4,3,2,1,0:T(8,128)S(1)}, u32[]{:S(2)}, u32[]{:S(2)}) collective-permute-start(f32[4,2,8,8,128]{4,3,2,1,0:T(8,128)S(1)} %collective-permute-done.12.refs_1_), channel_id=1, source_target_pairs={{0,0},{8,104},{16,16},{24,120},{32,32},{40,72},{48,48},{56,88},{64... | collective-permute-start | bytes 786440 | tf_op jit(solution)/shard_map/ppermute | solution.py:247
  63.9 7.1 %collective-permute-start.16 = (f32[4,2,8,8,128]{4,3,2,1,0:T(8,128)S(1)}, f32[4,2,8,8,128]{4,3,2,1,0:T(8,128)S(1)}, u32[]{:S(2)}, u32[]{:S(2)}) collective-permute-start(f32[4,2,8,8,128]{4,3,2,1,0:T(8,128)S(1)} %collective-permute-done.12.refs_1_), channel_id=1, source_target_pairs={{0,0},{8,40},{16,16},{24,56},{32,32},{40,8},{48,48},{56,24},{64,64... | collective-permute-start | bytes 786440 | tf_op jit(solution)/shard_map/ppermute | solution.py:247
  67.0 4.1 %collective-permute-start.25 = (f32[4,2,8,8,128]{4,3,2,1,0:T(8,128)S(1)}, f32[4,2,8,8,128]{4,3,2,1,0:T(8,128)S(1)}, u32[]{:S(2)}, u32[]{:S(2)}) collective-permute-start(f32[4,2,8,8,128]{4,3,2,1,0:T(8,128)S(1)} %collective-permute-done.18.refs_5_), channel_id=1, source_target_pairs={{0,8},{8,0},{16,24},{24,16},{32,40},{40,32},{48,56},{56,48},{64,72... | collective-permute-start | bytes 786440 | tf_op jit(solution)/shard_map/ppermute | solution.py:242
  67.1 4.0 %collective-permute-start.20 = (f32[4,2,8,8,128]{4,3,2,1,0:T(8,128)S(1)}, f32[4,2,8,8,128]{4,3,2,1,0:T(8,128)S(1)}, u32[]{:S(2)}, u32[]{:S(2)}) collective-permute-start(f32[4,2,8,8,128]{4,3,2,1,0:T(8,128)S(1)} %collective-permute-done.19.refs_14_), channel_id=1, source_target_pairs={{0,8},{8,0},{16,24},{24,16},{32,40},{40,32},{48,56},{56,48},{64,72... | collective-permute-start | bytes 786440 | tf_op jit(solution)/shard_map/ppermute | solution.py:242
  67.6 3.5 %collective-permute-start.15 = (f32[4,2,8,8,128]{4,3,2,1,0:T(8,128)S(1)}, f32[4,2,8,8,128]{4,3,2,1,0:T(8,128)S(1)}, u32[]{:S(2)}, u32[]{:S(2)}) collective-permute-start(f32[4,2,8,8,128]{4,3,2,1,0:T(8,128)S(1)} %collective-permute-done.14.refs_10_), channel_id=1, source_target_pairs={{0,8},{8,0},{16,24},{24,16},{32,40},{40,32},{48,56},{56,48},{64,72... | collective-permute-start | bytes 786440 | tf_op jit(solution)/shard_map/ppermute | solution.py:242
  69.6 1.5 %collective-permute-start.26 = (f32[4,2,8,8,128]{4,3,2,1,0:T(8,128)S(1)}, f32[4,2,8,8,128]{4,3,2,1,0:T(8,128)S(1)}, u32[]{:S(2)}, u32[]{:S(2)}) collective-permute-start(f32[4,2,8,8,128]{4,3,2,1,0:T(8,128)S(1)} %collective-permute-done.21.refs_7_), channel_id=1, source_target_pairs={{0,8},{8,0},{16,24},{24,16},{32,40},{40,32},{48,56},{56,48},{64,72... | collective-permute-start | bytes 786440 | tf_op jit(solution)/shard_map/ppermute | solution.py:242
  71.0 1.5 %collective-permute-start.23 = (f32[4,2,8,8,128]{4,3,2,1,0:T(8,128)S(1)}, f32[4,2,8,8,128]{4,3,2,1,0:T(8,128)S(1)}, u32[]{:S(2)}, u32[]{:S(2)}) collective-permute-start(f32[4,2,8,8,128]{4,3,2,1,0:T(8,128)S(1)} %collective-permute-done.16.refs_3_), channel_id=1, source_target_pairs={{0,8},{8,0},{16,24},{24,16},{32,40},{40,32},{48,56},{56,48},{64,72... | collective-permute-start | bytes 786440 | tf_op jit(solution)/shard_map/ppermute | solution.py:242
